TPU v7x, 32 devices: a whole 2x2x4 slice. The times are simulated.
32 devices in a mesh: row: 8 (over y, x, core), col: 4 (over z).
Axes of the slice: x: 2, y: 2, z: 4, core: 2. Of those that a mesh axis runs over, the one named last changes fastest.
Arguments:
- integrals: bfloat16 [320, 32, 4096], P('row', None, 'col'), may hold values from -6 to 6
- coeffs: bfloat16 [10240, 4096], P('row', 'col'), may hold values from -0.078125 to 0.078125
- mask: int32 [320, 4], replicated, may hold values from 0 to 1, as said below
- offsets: int32 [321], replicated, may hold values from 0 to 7680, as said below
- atom_of_slot: int32 [320], replicated, may hold values from 0 to 319, as said below
Outputs:
- half_transformed: bfloat16 [4096, 4096], P('row', 'col')
Inputs may be any that keep to these rules, and one draw needn't show every extreme that they name: `mask`: 1 marks a significant pair of an atom and a block of 64 window functions. offsets[0] = 0 and offsets[a + 1] - offsets[a] is atom a's number of basis functions, 16 to 32; atoms 2k and 2k + 1 together have 3 * 16; rows of an atom's padded block past its number are padding. `atom_of_slot`: a permutation of the atoms; slot k is held by atom owner k // 40 along row, and atom a's AO-row owner is a // 40; one atom owner holds at least one and at most 5 atoms of any one AO-row owner, and exactly 5 for some pairs.
All inputs are finite; a program needn't handle non-finite values.
Results may differ from a plain program's by a relative error of at most 0.015.
Values may be sent and summed in bfloat16 or wider, within the bound.
No kernel may reach another device: no remote copies, remote signals or barrier semaphores. Data moves between devices by JAX's collectives and lax.ppermute only.
A program may use at most 256 MiB of HBM per device.

v0:
```python
import jax
import jax.numpy as jnp
from jax import lax
from jax.sharding import PartitionSpec as P


def body(integrals, coeffs, mask, offsets, atom_of_slot):
    n_row = lax.axis_size("row")
    own_row = lax.axis_index("row")
    own_col = lax.axis_index("col")
    per_dev, atom_w, row_width = integrals.shape
    slots_cap = max(2, -(-per_dev // n_row))
    counter = jnp.arange(per_dev, dtype=jnp.int32)
    slot_count = n_row * slots_cap
    mine_slots = lax.dynamic_slice_in_dim(atom_of_slot, own_row * per_dev, per_dev)
    target = mine_slots // per_dev
    before = (target[None, :] == target[:, None]) & (counter[None, :] < counter[:, None])
    arrival_rank = jnp.sum(before.astype(jnp.int32), axis=1)
    position = target * slots_cap + arrival_rank
    placing = (jnp.arange(slot_count, dtype=jnp.int32)[:, None] == position[None, :]).astype(
        jnp.bfloat16
    )
    outgoing = jnp.dot(
        placing, integrals.reshape(per_dev, atom_w * row_width), preferred_element_type=jnp.bfloat16
    )
    outgoing = outgoing.reshape(n_row, slots_cap, atom_w * row_width)
    incoming = lax.all_to_all(outgoing, "row", split_axis=0, concat_axis=0, tiled=True)
    holders = atom_of_slot.reshape(n_row, per_dev)
    is_mine = holders // per_dev == own_row
    arrival = jnp.cumsum(is_mine.astype(jnp.int32), axis=1) - 1
    slot_of = jnp.arange(n_row, dtype=jnp.int32)[:, None] * slots_cap + arrival
    local_atom = holders - own_row * per_dev
    pick_atom = (
        (local_atom.reshape(-1)[:, None] == counter[None, :]) & is_mine.reshape(-1)[:, None]
    ).astype(jnp.float32)
    pick_slot = (
        slot_of.reshape(-1)[:, None] == jnp.arange(slot_count, dtype=jnp.int32)[None, :]
    ).astype(jnp.float32)
    gather_matrix = jnp.dot(pick_atom.T, pick_slot).astype(jnp.bfloat16)
    ordered = jnp.dot(
        gather_matrix,
        incoming.reshape(slot_count, atom_w * row_width),
        preferred_element_type=jnp.bfloat16,
    )
    ordered = ordered.reshape(per_dev, atom_w, row_width)
    bounds = lax.dynamic_slice_in_dim(offsets, own_row * per_dev, per_dev + 1)
    lengths = bounds[1:] - bounds[:-1]
    significant = lax.dynamic_slice(mask, (own_row * per_dev, own_col), (per_dev, 1))[:, 0] > 0
    keep_rows = (jnp.arange(atom_w, dtype=jnp.int32)[None, :] < lengths[:, None]) & significant[
        :, None
    ]
    blocks = ordered * keep_rows[:, :, None].astype(jnp.bfloat16)
    bucket_edges = [0, per_dev]
    kept_rows = blocks.reshape(per_dev * atom_w, row_width)
    coeff_piece = lax.all_gather(coeffs, "col", axis=1, tiled=True)
    low_row = bucket_edges[0] * atom_w
    high_row = bucket_edges[1] * atom_w

    def product(low_row=low_row, high_row=high_row):
        return lax.dot_general(
            coeff_piece, kept_rows, (((0,), (0,)), ((), ())), preferred_element_type=jnp.float32
        )

    bucket_term = product()
    partial_sums = bucket_term.astype(jnp.bfloat16)
    result = lax.psum_scatter(partial_sums, "row", scatter_dimension=0, tiled=True).astype(
        jnp.float32
    )
    return result.astype(jnp.bfloat16)


def solution(mesh):
    in_specs = (P("row", None, "col"), P("row", "col"), P(), P(), P())
    out_specs = P("row", "col")
    return jax.shard_map(body, mesh=mesh, in_specs=in_specs, out_specs=out_specs, check_vma=False)
```

profile of v0, /device:TPU:0, one launch (start us, length us, event | category | flops | bytes accessed | tf_op | source)
XLA Modules:
  0.0 291.5 jit_solution(10588621491693638440)
XLA Ops:
  6.5 0.7 all-gather.2.cloned.1.call-update
  7.3 3.9 %reshape.121 = bf16[40,32768,1]{1,0,2:T(8,128)(2,1)S(1)} reshape(bf16[40,32,1024]{2,1,0:T(8,128)(2,1)} %param.5) | data formatting | bytes 5242880 | tf_op jit(solution)/shard_map/reshape | solution.py:24
  11.2 0.1 and_select_fusion
  11.3 0.2 convert_reduce_fusion
  11.4 0.1 multiply_add_fusion.1
  11.5 0.1 broadcast_compare_fusion
  11.6 2.9 fusion.16
  14.5 5.2 %all-to-all-start = ((bf16[8,5,32768]{2,1,0:T(8,128)(2,1)}), bf16[8,5,32768]{2,1,0:T(8,128)(2,1)}, u32[]{:S(2)}, u32[]{:S(2)}) async-start(bf16[8,5,32768]{2,1,0:T(8,128)(2,1)} %fusion.16), calls=%async_computation | async-start | bytes 8388608 | tf_op jit(solution)/shard_map/all_to_all | solution.py:27
  19.7 0.1 and.41
  19.8 0.1 div.18
  19.9 0.2 reduce_window_sum.11
  20.1 0.1 add_add_fusion
  20.2 0.1 add.46
  20.3 0.8 dynamic_slice.10
  21.1 0.8 compare_bitcast_fusion
  21.8 0.1 slice_subtract_fusion
  21.9 47.0 %all-to-all-done = bf16[8,5,32768]{2,1,0:T(8,128)(2,1)} async-done(((bf16[8,5,32768]{2,1,0:T(8,128)(2,1)}), bf16[8,5,32768]{2,1,0:T(8,128)(2,1)}, u32[]{:S(2)}, u32[]{:S(2)}) %all-to-all-start) | async-done | bytes 2621472 | tf_op jit(solution)/shard_map/all_to_all | solution.py:27
  68.9 3.4 %reshape.119 = bf16[40,32768]{1,0:T(8,128)(2,1)S(1)} reshape(bf16[8,5,32768]{2,1,0:T(8,128)(2,1)} %all-to-all-done) | data formatting | bytes 5242880 | tf_op jit(solution)/shard_map/reshape | solution.py:42
  72.3 2.7 fusion.3
  75.0 3.2 %copy.17 = bf16[40,32,1024]{2,1,0:T(8,128)(2,1)S(1)} copy(bf16[40,32,1024]{2,0,1:T(8,128)(2,1)} %fusion.3) | data formatting | bytes 5242880 | tf_op jit(solution)/shard_map/mul | solution.py:52
  78.2 117.3 %all-gather.2.cloned.1.call-done = bf16[1280,4096]{1,0:T(8,128)(2,1)} async-done(((bf16[1280,1024]{1,0:T(8,128)(2,1)}), bf16[1280,4096]{1,0:T(8,128)(2,1)}) %all-gather.2.cloned.1.call-update) | async-done | bytes 10485776 | tf_op jit(solution)/shard_map/all_gather | solution.py:55
  195.6 17.2 %convert_bitcast_fusion = bf16[4096,1024]{0,1:T(8,128)(2,1)} fusion(bf16[1280,1024]{1,0:T(8,128)(2,1)S(1)} %bitcast.20, bf16[1280,4096]{1,0:T(8,128)(2,1)} %all-gather.2.cloned.1.call-done), kind=kOutput, calls=%fused_computation | convolution fusion | flops 10741612544 | bytes 21495808 | tf_op jit(solution)/shard_map/dot_general | solution.py:60
  212.8 69.6 %reduce-scatter.2.cloned.1.call-done = bf16[512,1024]{0,1:T(8,128)(2,1)} async-done(((bf16[4096,1024]{0,1:T(8,128)(2,1)}), bf16[512,1024]{0,1:T(8,128)(2,1)}) %reduce-scatter.2.cloned.1.call-update) | async-done | bytes 1048592 | tf_op jit(solution)/shard_map/reduce_scatter | solution.py:66
  282.4 2.3 copy.18
  (11 shorter events, 0.1 us)
Async XLA Ops:
  6.5 189.0 %all-gather.2.cloned.1.call-start = ((), (), s32[]{:S(2)}) async-start(), calls=%async_computation.2 | async-start | bytes 13107200 | tf_op jit(solution)/shard_map/all_gather | solution.py:55
  7.3 3.9 %copy-start = (s32[320]{0:T(512)S(1)}, s32[320]{0:T(512)}, u32[]{:S(2)}) copy-start(s32[320]{0:T(512)} %param.9) | copy-start | bytes 3844
  14.5 54.4 %all-to-all-start = ((bf16[8,5,32768]{2,1,0:T(8,128)(2,1)}), bf16[8,5,32768]{2,1,0:T(8,128)(2,1)}, u32[]{:S(2)}, u32[]{:S(2)}) async-start(bf16[8,5,32768]{2,1,0:T(8,128)(2,1)} %fusion.16), calls=%async_computation | async-start | bytes 8388608 | tf_op jit(solution)/shard_map/all_to_all | solution.py:27
  19.7 262.7 %reduce-scatter.2.cloned.1.call-start = ((), (), s32[]{:S(2)}) async-start(), calls=%async_computation.3 | async-start | bytes 9437184 | tf_op jit(solution)/shard_map/reduce_scatter | solution.py:66
Sparse Core Ops, SparseCore 0:
  8.9 186.6 all-gather.1
  212.9 69.4 reduce-scatter.1
where the time goes:
time: 292 us
  waiting for transfers between devices  235 us (80%)
  matrix products  22.8 us (8%)
  local copies, waits for them, and re-layouts  13.8 us (5%)
  between operations  13.5 us (5%)
  starting transfers between devices  5.24 us (2%)
    all_gather x1, waiting for transfers between devices, body(): coeff_piece = lax.all_gather(coeffs, 'col', axis=1, tiled=True)  117 us
    reduce_scatter x1, waiting for transfers between devices, body(): lax.psum_scatter(partial_sums, 'row', scatter_dimension=0, tiled=True)  69.6 us
    all_to_all x1, waiting for transfers between devices, body(): lax.all_to_all(outgoing, 'row', split_axis=0, concat_axis=0, tiled=True)  47 us
    dot_general x1, matrix products, product(): lax.dot_general(coeff_piece, kept_rows, (((0,), (0,)), ((), ())), preferr...  17.2 us
  transfers between devices with their start and end apart: 3, of which 3 were waited for; matrix products, arithmetic and copies ran while one was open for 6% of the time, Pallas kernels for 0%

commit v1 on v0

--- a/solution.py
+++ b/solution.py
@@ -1,7 +1,248 @@
+import functools
 import jax
 import jax.numpy as jnp
 from jax import lax
+from jax.experimental import pallas as pl
+from jax.experimental.pallas import tpu as pltpu
 from jax.sharding import PartitionSpec as P
+
+
+LANES = 256
+
+
+def selector(first, alive, atom_w, group):
+    pair_w = 3 * atom_w // 2
+    rows, cols = group // 2 * pair_w, group * atom_w
+    row = lax.broadcasted_iota(jnp.int32, (rows, cols), 0)
+    col = lax.broadcasted_iota(jnp.int32, (rows, cols), 1)
+    wanted = jnp.full((rows, cols), -1, jnp.int32)
+    for pair in range(group // 2):
+        inside = row - pair * pair_w
+        in_first = inside < first[pair]
+        source = jnp.where(in_first, inside, inside + atom_w - first[pair]) + 2 * pair * atom_w
+        if alive is not None:
+            live = jnp.where(in_first, alive[2 * pair], alive[2 * pair + 1]) > 0
+            source = jnp.where(live, source, -1)
+        wanted = jnp.where((inside >= 0) & (inside < pair_w), source, wanted)
+    return (wanted == col).astype(jnp.bfloat16)
+
+
+def pack_coeffs_kernel(atom_w, group, widths, lengths, core, coeffs, *pieces):
+    step = pl.program_id(0)
+    first = [lengths[step * group + 2 * pair] for pair in range(group // 2)]
+    chooser = selector(first, None, atom_w, group)
+    half = sum(widths)
+    for side in range(2):
+        start = half * jnp.where(core[0] == side, 0, 1)
+        for which, width in enumerate(widths):
+            offset = pl.multiple_of(start + sum(widths[:which]), 128)
+            block = coeffs[:, pl.ds(offset, width)]
+            pieces[side * len(widths) + which][...] = jnp.dot(
+                chooser, block, preferred_element_type=jnp.float32
+            ).astype(jnp.bfloat16)
+
+
+def pack_coeffs(coeffs, lengths, core, per_dev, atom_w, group, widths):
+    rows_in, rows_out = group * atom_w, group // 2 * (3 * atom_w // 2)
+    steps = per_dev // group
+    smem = pl.BlockSpec(memory_space=pltpu.SMEM)
+    return pl.pallas_call(
+        functools.partial(pack_coeffs_kernel, atom_w, group, widths),
+        grid=(steps,),
+        in_specs=[smem, smem, pl.BlockSpec((rows_in, coeffs.shape[1]), lambda i: (i, 0))],
+        out_specs=[pl.BlockSpec((rows_out, w), lambda i: (i, 0)) for w in widths * 2],
+        out_shape=[jax.ShapeDtypeStruct((steps * rows_out, w), jnp.bfloat16) for w in widths * 2],
+        name="pack_coeffs",
+    )(lengths, core, coeffs)
+
+
+def sort_blocks_kernel(slots, table, blocks, *outs):
+    for which, out in enumerate(outs):
+        for rank in range(2 * slots):
+            out[rank] = blocks[table[which * 2 * slots + rank]]
+
+
+def sort_blocks(blocks, table, n_chip, slots):
+    shape = (2 * slots,) + blocks.shape[1:]
+    vmem = pl.BlockSpec(memory_space=pltpu.VMEM)
+    return pl.pallas_call(
+        functools.partial(sort_blocks_kernel, slots),
+        in_specs=[pl.BlockSpec(memory_space=pltpu.SMEM), vmem],
+        out_specs=[vmem] * n_chip,
+        out_shape=[jax.ShapeDtypeStruct(shape, blocks.dtype)] * n_chip,
+        name="sort_blocks",
+    )(table, blocks)
+
+
+def pack_kept_kernel(n_in, slots, atom_w, group, where_of, lengths, alive, *refs):
+    arrived, out, stack, window = refs[:n_in], refs[n_in], refs[n_in + 1], refs[n_in + 2]
+    for which in range(n_in - 1):
+        stack[which * slots : (which + 1) * slots] = arrived[which][:slots]
+    stack[(n_in - 1) * slots :] = arrived[n_in - 1][...]
+    rows_out = group // 2 * (3 * atom_w // 2)
+    for step in range(out.shape[0] // rows_out):
+        base = step * group
+        for atom in range(group):
+            window[atom * atom_w : (atom + 1) * atom_w, :] = stack[where_of[base + atom]]
+        first = [lengths[base + 2 * pair] for pair in range(group // 2)]
+        chooser = selector(first, [alive[base + i] for i in range(group)], atom_w, group)
+        out[step * rows_out : (step + 1) * rows_out, :] = jnp.dot(
+            chooser, window[...], preferred_element_type=jnp.float32
+        ).astype(jnp.bfloat16)
+
+
+def pack_kept(arrived, where_of, lengths, alive, atom_w, group):
+    slots, width = arrived[0].shape[0] // 2, arrived[0].shape[2]
+    per_dev = where_of.shape[0]
+    smem, vmem = pl.BlockSpec(memory_space=pltpu.SMEM), pl.BlockSpec(memory_space=pltpu.VMEM)
+    return pl.pallas_call(
+        functools.partial(pack_kept_kernel, len(arrived), slots, atom_w, group),
+        in_specs=[smem] * 3 + [vmem] * len(arrived),
+        out_specs=vmem,
+        out_shape=jax.ShapeDtypeStruct((per_dev // 2 * (3 * atom_w // 2), width), jnp.bfloat16),
+        scratch_shapes=[
+            pltpu.VMEM((per_dev, atom_w, width), jnp.bfloat16),
+            pltpu.VMEM((group * atom_w, width), jnp.bfloat16),
+        ],
+        name="pack_kept",
+    )(where_of, lengths, alive, *arrived)
+
+
+def block_tables(atom_of_slot, own_row, n_row, per_dev, slots):
+    counter = jnp.arange(per_dev, dtype=jnp.int32)
+    holders = atom_of_slot.reshape(n_row, per_dev)
+    owner = holders // per_dev
+    earlier = (owner[:, None, :] == owner[:, :, None]) & (counter[None, :] < counter[:, None])[None]
+    rank = jnp.sum(earlier.astype(jnp.int32), axis=2)
+    mine_owner = lax.dynamic_slice_in_dim(owner, own_row, 1)[0]
+    mine_rank = lax.dynamic_slice_in_dim(rank, own_row, 1)[0]
+    place = (mine_owner ^ own_row) * slots + mine_rank
+    table = jnp.sum(jnp.where(place[None, :] == counter[:, None], counter[None, :], 0), axis=1)
+    apart = jnp.arange(n_row, dtype=jnp.int32)[:, None] ^ own_row
+    arrival = ((apart % 2) * (n_row // 2) + apart // 2) * slots + rank
+    local = holders.reshape(-1) - own_row * per_dev
+    where_of = jnp.sum(
+        jnp.where(local[None, :] == counter[:, None], arrival.reshape(-1)[None, :], 0), axis=1
+    )
+    return table, where_of
+
+
+def products_kernel(n_stream, choice, kept, kept_pair, *refs):
+    streams, outs = refs[:n_stream], refs[n_stream : n_stream + len(refs) - n_stream - 2]
+    buffer, sems = refs[-2], refs[-1]
+    width = outs[0].shape[0]
+
+    def fetch(step):
+        for which in range(n_stream):
+
+            @pl.when(choice[step] == which)
+            def _():
+                pltpu.make_async_copy(
+                    streams[which], buffer.at[step % 2], sems.at[step % 2]
+                ).start()
+
+    fetch(0)
+    for step, out in enumerate(outs):
+        if step + 1 < len(outs):
+            fetch(step + 1)
+        pltpu.make_async_copy(streams[0], buffer.at[step % 2], sems.at[step % 2]).wait()
+        dims = (((0,), (0,)), ((), ()))
+        total = lax.dot_general(
+            buffer[step % 2, :, :width], kept[...], dims, preferred_element_type=jnp.float32
+        )
+        total += lax.dot_general(
+            buffer[step % 2, :, width:], kept_pair[...], dims, preferred_element_type=jnp.float32
+        )
+        out[...] = total.astype(out.dtype)
+
+
+def products(choice, kept, kept_pair, streams, n_out):
+    rows, both = streams[0].shape
+    width, columns = both // 2, kept.shape[1]
+    vmem = pl.BlockSpec(memory_space=pltpu.VMEM)
+    flops = n_out * 2 * both * rows * columns
+    return pl.pallas_call(
+        functools.partial(products_kernel, len(streams)),
+        in_specs=[pl.BlockSpec(memory_space=pltpu.SMEM), vmem, vmem]
+        + [pl.BlockSpec(memory_space=pl.ANY)] * len(streams),
+        out_specs=[vmem] * n_out,
+        out_shape=[jax.ShapeDtypeStruct((width, columns), jnp.bfloat16)] * n_out,
+        scratch_shapes=[
+            pltpu.VMEM((2, rows, both), jnp.bfloat16),
+            pltpu.SemaphoreType.DMA((2,)),
+        ],
+        cost_estimate=pl.CostEstimate(flops=flops, bytes_accessed=flops // 512, transcendentals=0),
+        name="products",
+    )(choice, kept, kept_pair, *streams)
+
+
+def line_body(integrals, coeffs, mask, offsets, atom_of_slot):
+    n_row, n_col = lax.axis_size("row"), lax.axis_size("col")
+    own_row, own_col = lax.axis_index("row"), lax.axis_index("col")
+    per_dev, atom_w, _ = integrals.shape
+    slots = per_dev // n_row
+    group = LANES // atom_w
+    core, chip = own_row % 2, own_row // 2
+    n_chip = n_row // 2
+    half = coeffs.shape[1] // 2
+    widths = (half // 2, half // 4, half // 4)
+    n_piece = len(widths)
+
+    bounds = lax.dynamic_slice_in_dim(offsets, own_row * per_dev, per_dev + 1)
+    lengths = bounds[1:] - bounds[:-1]
+    core_arg = core.astype(jnp.int32).reshape(1)
+
+    swap = [(r, r ^ 1) for r in range(n_row)]
+    pieces = pack_coeffs(coeffs, lengths, core_arg, per_dev, atom_w, group, (half,))
+    paired = lax.ppermute(pieces[1], "row", swap)
+    units = []
+    for which in range(n_piece):
+        cut = slice(sum(widths[:which]), sum(widths[: which + 1]))
+        units.append(jnp.concatenate([pieces[0][:, cut], paired[:, cut]], axis=1))
+
+    right = [(c, c + 1) for c in range(n_col - 1)]
+    left = [(c + 1, c) for c in range(n_col - 1)]
+    from_left = [lax.ppermute(unit, "col", right) for unit in units]
+    from_right = [lax.ppermute(unit, "col", left) for unit in units]
+
+    table, where_of = block_tables(atom_of_slot, own_row, n_row, per_dev, slots)
+    alive = lax.dynamic_slice(mask, (own_row * per_dev, own_col), (per_dev, 1))[:, 0]
+    outgoing = sort_blocks(integrals, table, n_chip, slots)
+    arrived = [outgoing[0]] + [
+        lax.ppermute(outgoing[d], "row", [(r, r ^ (2 * d)) for r in range(n_row)])
+        for d in range(1, n_chip)
+    ]
+    theirs = jnp.concatenate([block[slots:] for block in arrived], axis=0)
+    arrived.append(lax.ppermute(theirs, "row", swap))
+    kept = pack_kept(arrived, where_of, lengths, alive, atom_w, group)
+    kept_pair = lax.ppermute(kept, "row", swap)
+
+    far_left = [lax.ppermute(unit, "col", right[1:]) for unit in from_left]
+    far_right = [lax.ppermute(unit, "col", left[:-1]) for unit in from_right]
+    on_left = own_col < n_col // 2
+    third = [
+        lax.ppermute(jnp.where(on_left, r, l), "col", [(1, 0), (n_col - 2, n_col - 1)])
+        for l, r in zip(far_left, far_right)
+    ]
+
+    goals = chip ^ jnp.arange(n_chip, dtype=jnp.int32)
+    gap = goals - own_col
+    choice = jnp.full((n_chip,), 5, jnp.int32)
+    for value, which in ((0, 0), (-1, 1), (1, 2), (-2, 3), (2, 4)):
+        choice = jnp.where(gap == value, which, choice)
+    rows = []
+    for which in range(n_piece):
+        streams = [
+            group_of[which]
+            for group_of in (units, from_left, from_right, far_left, far_right, third)
+        ]
+        parts = products(choice, kept, kept_pair, streams, n_chip)
+        total = parts[0].astype(jnp.float32)
+        for d in range(1, n_chip):
+            perm = [(r, r ^ (2 * d)) for r in range(n_row)]
+            total = total + lax.ppermute(parts[d], "row", perm).astype(jnp.float32)
+        rows.append(total.astype(jnp.bfloat16))
+    return jnp.concatenate(rows, axis=0)
 
 
 def body(integrals, coeffs, mask, offsets, atom_of_slot):
@@ -50,13 +291,10 @@
         :, None
     ]
     blocks = ordered * keep_rows[:, :, None].astype(jnp.bfloat16)
-    bucket_edges = [0, per_dev]
     kept_rows = blocks.reshape(per_dev * atom_w, row_width)
     coeff_piece = lax.all_gather(coeffs, "col", axis=1, tiled=True)
-    low_row = bucket_edges[0] * atom_w
-    high_row = bucket_edges[1] * atom_w
-
-    def product(low_row=low_row, high_row=high_row):
+
+    def product():
         return lax.dot_general(
             coeff_piece, kept_rows, (((0,), (0,)), ((), ())), preferred_element_type=jnp.float32
         )
@@ -72,4 +310,14 @@
 def solution(mesh):
     in_specs = (P("row", None, "col"), P("row", "col"), P(), P(), P())
     out_specs = P("row", "col")
-    return jax.shard_map(body, mesh=mesh, in_specs=in_specs, out_specs=out_specs, check_vma=False)
+    n_row, n_col = mesh.shape["row"], mesh.shape["col"]
+
+    def step(integrals, coeffs, mask, offsets, atom_of_slot):
+        even = integrals.shape[0] % (n_row * n_row) == 0
+        chosen = line_body if even and n_col == 4 and n_row == 2 * n_col else body
+        mapped = jax.shard_map(
+            chosen, mesh=mesh, in_specs=in_specs, out_specs=out_specs, check_vma=False
+        )
+        return mapped(integrals, coeffs, mask, offsets, atom_of_slot)
+
+    return step

time: 292 us -> 238 us (0.82)
  waiting for transfers between devices: 235 us -> 137 us
  starting transfers between devices: 5.24 us -> 45 us
  Pallas kernels: 0 us -> 35.8 us
  matrix products: 22.8 us -> 0 us
  between operations: 13.5 us -> 0.47 us
  other arithmetic: 1.59 us -> 11.2 us
  local copies, waits for them, and re-layouts: 13.8 us -> 7.64 us
    ppermute x0 -> x30, waiting for transfers between devices: none -> 137 us  [the longest x3 28.7 us: line_body(): lax.ppermute(jnp.where(on_left, r, l), 'col', [(1, 0), (n_col - 2, n_col...]
    all_gather x1 -> x0, waiting for transfers between devices: 117 us -> none  [body(): coeff_piece = lax.all_gather(coeffs, 'col', axis=1, tiled=True)]
    reduce_scatter x1 -> x0, waiting for transfers between devices: 69.6 us -> none  [body(): lax.psum_scatter(partial_sums, 'row', scatter_dimension=0, tiled=True)]
    all_to_all x1 -> x0, waiting for transfers between devices: 47 us -> none  [body(): lax.all_to_all(outgoing, 'row', split_axis=0, concat_axis=0, tiled=True)]
    ppermute x0 -> x30, starting transfers between devices: none -> 45 us  [the longest x3 15.2 us: line_body(): from_left = [lax.ppermute(unit, 'col', right) for unit in units]]
    pallas_call x0 -> x6, Pallas kernels: none -> 35.8 us  [the longest x3 23 us: products(): pl.pallas_call(functools.partial(products_kernel, len(streams)), in_specs...]
    dot_general x3 -> x0, matrix products: 22.8 us -> none  [the longest x1 17.2 us: product(): lax.dot_general(coeff_piece, kept_rows, (((0,), (0,)), ((), ())), preferr...]
    reshape x2 -> x0, local copies, waits for them, and re-layouts: 7.29 us -> none  [the longest x1 3.88 us: body(): integrals.reshape(per_dev, atom_w * row_width)]
  transfers between devices with their start and end apart: 3 -> 30, of which waited for: 3 -> 11; matrix products, arithmetic and copies ran while one was open for 6% -> 6% of each run, Pallas kernels for 0% -> 13%
where the time goes in v1:
time: 238 us; the launch traced here: 237 us
  waiting for transfers between devices  137 us (58%)
  starting transfers between devices  45 us (19%)
  Pallas kernels  35.8 us (15%)
  other arithmetic  11.2 us (5%)
  local copies, waits for them, and re-layouts  7.64 us (3%)
    ppermute x3, waiting for transfers between devices, line_body(): lax.ppermute(jnp.where(on_left, r, l), 'col', [(1, 0), (n_col - 2, n_col...  28.7 us
    ppermute x3, waiting for transfers between devices, line_body(): lax.ppermute(outgoing[d], 'row', [(r, r ^ 2 * d) for r in range(n_row)])  28.3 us
    pallas_call x3, Pallas kernels, products(): pl.pallas_call(functools.partial(products_kernel, len(streams)), in_specs...  23 us
    ppermute x9, waiting for transfers between devices, line_body(): total = total + lax.ppermute(parts[d], 'row', perm).astype(jnp.float32)  22.9 us
    ppermute x3, waiting for transfers between devices, line_body(): from_right = [lax.ppermute(unit, 'col', left) for unit in units]  19.8 us
    ppermute x3, waiting for transfers between devices, line_body(): from_left = [lax.ppermute(unit, 'col', right) for unit in units]  19.5 us
    ppermute x3, waiting for transfers between devices, line_body(): far_right = [lax.ppermute(unit, 'col', left[:-1]) for unit in from_right]  17.6 us
    ppermute x3, starting transfers between devices, line_body(): from_left = [lax.ppermute(unit, 'col', right) for unit in units]  15.2 us
  transfers between devices with their start and end apart: 30, of which 11 were waited for; matrix products, arithmetic and copies ran while one was open for 6% of the time, Pallas kernels for 13%

profile of v1, /device:TPU:0, one launch (start us, length us, event | category | flops | bytes accessed | tf_op | source)
XLA Modules:
  0.0 236.9 jit_solution(14574520662219242631)
XLA Ops:
  1.5 4.9 %pack_coeffs.1 = (bf16[960,512]{1,0:T(8,128)(2,1)}, bf16[960,512]{1,0:T(8,128)(2,1)}) custom-call(s32[40]{0:T(128)} %slice_subtract_fusion.lengths, s32[1]{0:T(128)} %bitcast.2.core, bf16[1280,1024]{1,0:T(8,128)(2,1)} %coeffs.1), custom_call_target="tpu_custom_call" | custom-call | tf_op jit(solution)/shard_map/pack_coeffs/pallas_call | solution.py:49
  8.1 3.5 %sort_blocks.1 = (bf16[10,32,1024]{2,1,0:T(8,128)(2,1)}, bf16[10,32,1024]{2,1,0:T(8,128)(2,1)}, bf16[10,32,1024]{2,1,0:T(8,128)(2,1)}, bf16[10,32,1024]{2,1,0:T(8,128)(2,1)}) custom-call(s32[40]{0:T(128)} %select_reduce_fusion.1.table, bf16[40,32,1024]{2,1,0:T(8,128)(2,1)} %blocks.1), custom_call_target="tpu_custom_call" | custom-call | tf_op jit(solution)/shard_map/sort_blocks/pallas_call | solution.py:68
  11.6 3.4 %collective-permute-start.2 = (bf16[10,32,1024]{2,1,0:T(8,128)(2,1)}, bf16[10,32,1024]{2,1,0:T(8,128)(2,1)S(1)}, u32[]{:S(2)}, u32[]{:S(2)}) collective-permute-start(bf16[10,32,1024]{2,1,0:T(8,128)(2,1)} %get-tuple-element.26), channel_id=1, source_target_pairs={{0,24},{4,28},{8,16},{12,20},{16,8},{20,12},{24,0},{28,4},{1,25},{... | collective-permute-start | bytes 1966088 | tf_op jit(solution)/shard_map/ppermute | solution.py:212
  16.6 14.2 %collective-permute-done.2.refs_3_ = bf16[10,32,1024]{2,1,0:T(8,128)(2,1)S(1)} collective-permute-done((bf16[10,32,1024]{2,1,0:T(8,128)(2,1)}, bf16[10,32,1024]{2,1,0:T(8,128)(2,1)S(1)}, u32[]{:S(2)}, u32[]{:S(2)}) %collective-permute-start.2) | collective-permute-done | bytes 655392 | tf_op jit(solution)/shard_map/ppermute | solution.py:212
  30.9 13.8 %collective-permute-done.1.refs_2_ = bf16[10,32,1024]{2,1,0:T(8,128)(2,1)S(1)} collective-permute-done((bf16[10,32,1024]{2,1,0:T(8,128)(2,1)}, bf16[10,32,1024]{2,1,0:T(8,128)(2,1)S(1)}, u32[]{:S(2)}, u32[]{:S(2)}) %collective-permute-start.1) | collective-permute-done | bytes 655392 | tf_op jit(solution)/shard_map/ppermute | solution.py:212
  47.5 4.6 %collective-permute-start.6 = (bf16[960,512]{1,0:T(8,128)(2,1)S(1)}, bf16[960,512]{1,0:T(8,128)(2,1)}, u32[]{:S(2)}, u32[]{:S(2)}) collective-permute-start(bf16[960,512]{1,0:T(8,128)(2,1)S(1)} %pad_maximum_fusion.2.refs_0_), channel_id=1, source_target_pairs={{0,1},{1,2},{2,3},{4,5},{5,6},{6,7},{8,9},{9,10},{10,11},{12,13},{... | collective-permute-start | bytes 2949128 | tf_op jit(solution)/shard_map/ppermute | solution.py:205
  53.5 1.8 fusion.5
  56.1 5.3 %collective-permute-start.22 = (bf16[960,256]{1,0:T(8,128)(2,1)}, bf16[960,256]{1,0:T(8,128)(2,1)}, u32[]{:S(2)}, u32[]{:S(2)}) collective-permute-start(bf16[960,256]{1,0:T(8,128)(2,1)} %pad_maximum_fusion.4.refs_0_), channel_id=1, source_target_pairs={{0,1},{1,2},{2,3},{4,5},{5,6},{6,7},{8,9},{9,10},{10,11},{12,13},{... | collective-permute-start | bytes 1474568 | tf_op jit(solution)/shard_map/ppermute | solution.py:205
  62.8 10.5 %collective-permute-done.6.refs_1_ = bf16[960,512]{1,0:T(8,128)(2,1)} collective-permute-done((bf16[960,512]{1,0:T(8,128)(2,1)S(1)}, bf16[960,512]{1,0:T(8,128)(2,1)}, u32[]{:S(2)}, u32[]{:S(2)}) %collective-permute-start.6) | collective-permute-done | bytes 983072 | tf_op jit(solution)/shard_map/ppermute | solution.py:205
  74.0 4.7 %collective-permute-done.7.refs_2_ = bf16[960,512]{1,0:T(8,128)(2,1)} collective-permute-done((bf16[960,512]{1,0:T(8,128)(2,1)S(1)}, bf16[960,512]{1,0:T(8,128)(2,1)}, u32[]{:S(2)}, u32[]{:S(2)}) %collective-permute-start.7) | collective-permute-done | bytes 983072 | tf_op jit(solution)/shard_map/ppermute | solution.py:206
  82.4 4.3 %pack_kept.1.kept = bf16[960,1024]{1,0:T(8,128)(2,1)} custom-call(s32[40]{0:T(128)} %select_reduce_fusion.where_of, s32[40]{0:T(128)} %slice_subtract_fusion.lengths, s32[40]{0:T(128)} %dynamic-slice_bitcast_fusion.alive, bf16[10,32,1024]{2,1,0:T(8,128)(2,1)} %get-tuple-element.23.refs_0_, bf16[10,32,1024]{2,1,0:T(8,128)(2,1)} %copy-done.3, ...), custom_call_target="tpu_custom_call" | custom-call | tf_op jit(solution)/shard_map/pack_kept/pallas_call | solution.py:98
  87.8 5.3 %collective-permute-start.14 = (bf16[960,256]{1,0:T(8,128)(2,1)S(1)}, bf16[960,256]{1,0:T(8,128)(2,1)}, u32[]{:S(2)}, u32[]{:S(2)}) collective-permute-start(bf16[960,256]{1,0:T(8,128)(2,1)S(1)} %pad_maximum_fusion.3.refs_0_), channel_id=1, source_target_pairs={{0,1},{1,2},{2,3},{4,5},{5,6},{6,7},{8,9},{9,10},{10,11},{12,13},{... | collective-permute-start | bytes 1474568 | tf_op jit(solution)/shard_map/ppermute | solution.py:205
  94.4 9.1 %collective-permute-done.14.refs_1_ = bf16[960,256]{1,0:T(8,128)(2,1)} collective-permute-done((bf16[960,256]{1,0:T(8,128)(2,1)S(1)}, bf16[960,256]{1,0:T(8,128)(2,1)}, u32[]{:S(2)}, u32[]{:S(2)}) %collective-permute-start.14) | collective-permute-done | bytes 491552 | tf_op jit(solution)/shard_map/ppermute | solution.py:205
  104.9 15.1 %collective-permute-done.15.refs_2_ = bf16[960,256]{1,0:T(8,128)(2,1)} collective-permute-done((bf16[960,256]{1,0:T(8,128)(2,1)S(1)}, bf16[960,256]{1,0:T(8,128)(2,1)}, u32[]{:S(2)}, u32[]{:S(2)}) %collective-permute-start.15) | collective-permute-done | bytes 491552 | tf_op jit(solution)/shard_map/ppermute | solution.py:206
  125.9 10.3 %collective-permute-done.25.refs_4_ = bf16[960,256]{1,0:T(8,128)(2,1)} collective-permute-done((bf16[960,256]{1,0:T(8,128)(2,1)}, bf16[960,256]{1,0:T(8,128)(2,1)}, u32[]{:S(2)}, u32[]{:S(2)}) %collective-permute-start.25) | collective-permute-done | bytes 491552 | tf_op jit(solution)/shard_map/ppermute | solution.py:221
  136.3 1.9 broadcast_select_fusion.1
  139.5 7.2 %collective-permute-done.17.refs_4_ = bf16[960,256]{1,0:T(8,128)(2,1)S(1)} collective-permute-done((bf16[960,256]{1,0:T(8,128)(2,1)}, bf16[960,256]{1,0:T(8,128)(2,1)S(1)}, u32[]{:S(2)}, u32[]{:S(2)}) %collective-permute-start.17) | collective-permute-done | bytes 491552 | tf_op jit(solution)/shard_map/ppermute | solution.py:221
  149.7 28.7 %collective-permute-done.26.refs_5_ = bf16[960,256]{1,0:T(8,128)(2,1)} collective-permute-done((bf16[960,256]{1,0:T(8,128)(2,1)}, bf16[960,256]{1,0:T(8,128)(2,1)}, u32[]{:S(2)}, u32[]{:S(2)}) %collective-permute-start.26) | collective-permute-done | bytes 491552 | tf_op jit(solution)/shard_map/ppermute | solution.py:224
  178.4 6.9 %products.5 = (bf16[128,1024]{1,0:T(8,128)(2,1)}, bf16[128,1024]{1,0:T(8,128)(2,1)}, bf16[128,1024]{1,0:T(8,128)(2,1)}, bf16[128,1024]{1,0:T(8,128)(2,1)}) custom-call(s32[4]{0:T(128)} %compare_select_fusion.4.choice, bf16[960,1024]{1,0:T(8,128)(2,1)} %pack_kept.1.kept, bf16[960,1024]{1,0:T(8,128)(2,1)} %collective-permute-done.4.kept_pair, ...), custom_call_target="tpu_custom_call" | custom-call | flops 2013265920 | bytes 3932160 | tf_op jit(solution)/shard_map/products/pallas_call | solution.py:164
  185.3 1.8 collective-permute-start.29
  188.9 6.9 %products.4 = (bf16[128,1024]{1,0:T(8,128)(2,1)}, bf16[128,1024]{1,0:T(8,128)(2,1)}, bf16[128,1024]{1,0:T(8,128)(2,1)}, bf16[128,1024]{1,0:T(8,128)(2,1)}) custom-call(s32[4]{0:T(128)} %compare_select_fusion.4.choice, bf16[960,1024]{1,0:T(8,128)(2,1)} %pack_kept.1.kept, bf16[960,1024]{1,0:T(8,128)(2,1)} %collective-permute-done.4.kept_pair, ...), custom_call_target="tpu_custom_call" | custom-call | flops 2013265920 | bytes 3932160 | tf_op jit(solution)/shard_map/products/pallas_call | solution.py:164
  195.8 1.8 collective-permute-start.21
  197.6 9.3 %products.3 = (bf16[256,1024]{1,0:T(8,128)(2,1)}, bf16[256,1024]{1,0:T(8,128)(2,1)}, bf16[256,1024]{1,0:T(8,128)(2,1)}, bf16[256,1024]{1,0:T(8,128)(2,1)}) custom-call(s32[4]{0:T(128)} %compare_select_fusion.4.choice, bf16[960,1024]{1,0:T(8,128)(2,1)} %pack_kept.1.kept, bf16[960,1024]{1,0:T(8,128)(2,1)} %collective-permute-done.4.kept_pair, ...), custom_call_target="tpu_custom_call" | custom-call | flops 4026531840 | bytes 7864320 | tf_op jit(solution)/shard_map/products/pallas_call | solution.py:164
  212.4 22.9 %collective-permute-done.20 = bf16[128,1024]{1,0:T(8,128)(2,1)S(1)} collective-permute-done((bf16[128,1024]{1,0:T(8,128)(2,1)S(1)}, bf16[128,1024]{1,0:T(8,128)(2,1)S(1)}, u32[]{:S(2)}, u32[]{:S(2)}) %collective-permute-start.20) | collective-permute-done | bytes 262176 | tf_op jit(solution)/shard_map/ppermute | solution.py:243
  (114 shorter events, 38.2 us)
Async XLA Ops:
  6.4 39.9 %collective-permute-start.5 = (bf16[960,512]{1,0:T(8,128)(2,1)}, bf16[960,512]{1,0:T(8,128)(2,1)}, u32[]{:S(2)}, u32[]{:S(2)}) collective-permute-start(bf16[960,512]{1,0:T(8,128)(2,1)} %get-tuple-element.28), channel_id=1, source_target_pairs={{0,4},{4,0},{8,12},{12,8},{16,20},{20,16},{24,28},{28,24},{1,5},{5... | collective-permute-start | bytes 2949128 | tf_op jit(solution)/shard_map/ppermute | solution.py:197
  15.0 29.6 %collective-permute-start.1 = (bf16[10,32,1024]{2,1,0:T(8,128)(2,1)}, bf16[10,32,1024]{2,1,0:T(8,128)(2,1)S(1)}, u32[]{:S(2)}, u32[]{:S(2)}) collective-permute-start(bf16[10,32,1024]{2,1,0:T(8,128)(2,1)} %get-tuple-element.25), channel_id=1, source_target_pairs={{0,16},{4,20},{8,24},{12,28},{16,0},{20,4},{24,8},{28,12},{1,17},{... | collective-permute-start | bytes 1966088 | tf_op jit(solution)/shard_map/ppermute | solution.py:212
  15.5 29.4 %collective-permute-start = (bf16[10,32,1024]{2,1,0:T(8,128)(2,1)}, bf16[10,32,1024]{2,1,0:T(8,128)(2,1)S(1)}, u32[]{:S(2)}, u32[]{:S(2)}) collective-permute-start(bf16[10,32,1024]{2,1,0:T(8,128)(2,1)} %get-tuple-element.24), channel_id=1, source_target_pairs={{0,8},{4,12},{8,0},{12,4},{16,24},{20,28},{24,16},{28,20},{1,9},{5... | collective-permute-start | bytes 1966088 | tf_op jit(solution)/shard_map/ppermute | solution.py:212
  46.3 35.1 %collective-permute-start.3 = (bf16[20,32,1024]{2,1,0:T(8,128)(2,1)}, bf16[20,32,1024]{2,1,0:T(8,128)(2,1)S(1)}, u32[]{:S(2)}, u32[]{:S(2)}) collective-permute-start(bf16[20,32,1024]{2,1,0:T(8,128)(2,1)} %pad_maximum_fusion), channel_id=1, source_target_pairs={{0,4},{4,0},{8,12},{12,8},{16,20},{20,16},{24,28},{28,24},{1,5},{5... | collective-permute-start | bytes 3932168 | tf_op jit(solution)/shard_map/ppermute | solution.py:216
  47.5 25.7 %collective-permute-start.6 = (bf16[960,512]{1,0:T(8,128)(2,1)S(1)}, bf16[960,512]{1,0:T(8,128)(2,1)}, u32[]{:S(2)}, u32[]{:S(2)}) collective-permute-start(bf16[960,512]{1,0:T(8,128)(2,1)S(1)} %pad_maximum_fusion.2.refs_0_), channel_id=1, source_target_pairs={{0,1},{1,2},{2,3},{4,5},{5,6},{6,7},{8,9},{9,10},{10,11},{12,13},{... | collective-permute-start | bytes 2949128 | tf_op jit(solution)/shard_map/ppermute | solution.py:205
  52.1 26.6 %collective-permute-start.7 = (bf16[960,512]{1,0:T(8,128)(2,1)S(1)}, bf16[960,512]{1,0:T(8,128)(2,1)}, u32[]{:S(2)}, u32[]{:S(2)}) collective-permute-start(bf16[960,512]{1,0:T(8,128)(2,1)S(1)} %pad_maximum_fusion.2.refs_0_), channel_id=1, source_target_pairs={{1,0},{2,1},{3,2},{5,4},{6,5},{7,6},{9,8},{10,9},{11,10},{13,12},{... | collective-permute-start | bytes 2949128 | tf_op jit(solution)/shard_map/ppermute | solution.py:206
  56.1 31.6 %collective-permute-start.22 = (bf16[960,256]{1,0:T(8,128)(2,1)}, bf16[960,256]{1,0:T(8,128)(2,1)}, u32[]{:S(2)}, u32[]{:S(2)}) collective-permute-start(bf16[960,256]{1,0:T(8,128)(2,1)} %pad_maximum_fusion.4.refs_0_), channel_id=1, source_target_pairs={{0,1},{1,2},{2,3},{4,5},{5,6},{6,7},{8,9},{9,10},{10,11},{12,13},{... | collective-permute-start | bytes 1474568 | tf_op jit(solution)/shard_map/ppermute | solution.py:205
  61.5 31.6 %collective-permute-start.23 = (bf16[960,256]{1,0:T(8,128)(2,1)}, bf16[960,256]{1,0:T(8,128)(2,1)}, u32[]{:S(2)}, u32[]{:S(2)}) collective-permute-start(bf16[960,256]{1,0:T(8,128)(2,1)} %pad_maximum_fusion.4.refs_0_), channel_id=1, source_target_pairs={{1,0},{2,1},{3,2},{5,4},{6,5},{7,6},{9,8},{10,9},{11,10},{13,12},{... | collective-permute-start | bytes 1474568 | tf_op jit(solution)/shard_map/ppermute | solution.py:206
  73.3 48.0 %collective-permute-start.8 = (bf16[960,512]{1,0:T(8,128)(2,1)}, bf16[960,512]{1,0:T(8,128)(2,1)S(1)}, u32[]{:S(2)}, u32[]{:S(2)}) collective-permute-start(bf16[960,512]{1,0:T(8,128)(2,1)} %collective-permute-done.6.refs_1_), channel_id=1, source_target_pairs={{1,2},{2,3},{5,6},{6,7},{9,10},{10,11},{13,14},{14,15},{17,18},{18... | collective-permute-start | bytes 2949128 | tf_op jit(solution)/shard_map/ppermute | solution.py:220
  78.7 43.3 %collective-permute-start.9 = (bf16[960,512]{1,0:T(8,128)(2,1)}, bf16[960,512]{1,0:T(8,128)(2,1)}, u32[]{:S(2)}, u32[]{:S(2)}) collective-permute-start(bf16[960,512]{1,0:T(8,128)(2,1)} %collective-permute-done.7.refs_2_), channel_id=1, source_target_pairs={{1,0},{2,1},{5,4},{6,5},{9,8},{10,9},{13,12},{14,13},{17,16},{18,1... | collective-permute-start | bytes 2949128 | tf_op jit(solution)/shard_map/ppermute | solution.py:221
  86.7 91.7 %collective-permute-start.4 = (bf16[960,1024]{1,0:T(8,128)(2,1)}, bf16[960,1024]{1,0:T(8,128)(2,1)}, u32[]{:S(2)}, u32[]{:S(2)}) collective-permute-start(bf16[960,1024]{1,0:T(8,128)(2,1)} %pack_kept.1.kept), channel_id=1, source_target_pairs={{0,4},{4,0},{8,12},{12,8},{16,20},{20,16},{24,28},{28,24},{1,5},{5... | collective-permute-start | bytes 5898248 | tf_op jit(solution)/shard_map/ppermute | solution.py:218
  93.1 26.9 %collective-permute-start.15 = (bf16[960,256]{1,0:T(8,128)(2,1)S(1)}, bf16[960,256]{1,0:T(8,128)(2,1)}, u32[]{:S(2)}, u32[]{:S(2)}) collective-permute-start(bf16[960,256]{1,0:T(8,128)(2,1)S(1)} %pad_maximum_fusion.3.refs_0_), channel_id=1, source_target_pairs={{1,0},{2,1},{3,2},{5,4},{6,5},{7,6},{9,8},{10,9},{11,10},{13,12},{... | collective-permute-start | bytes 1474568 | tf_op jit(solution)/shard_map/ppermute | solution.py:206
  122.0 24.7 %collective-permute-start.17 = (bf16[960,256]{1,0:T(8,128)(2,1)}, bf16[960,256]{1,0:T(8,128)(2,1)S(1)}, u32[]{:S(2)}, u32[]{:S(2)}) collective-permute-start(bf16[960,256]{1,0:T(8,128)(2,1)} %collective-permute-done.15.refs_2_), channel_id=1, source_target_pairs={{1,0},{2,1},{5,4},{6,5},{9,8},{10,9},{13,12},{14,13},{17,16},{18,1... | collective-permute-start | bytes 1474568 | tf_op jit(solution)/shard_map/ppermute | solution.py:221
  124.6 72.9 %collective-permute-start.10 = (bf16[960,512]{1,0:T(8,128)(2,1)S(1)}, bf16[960,512]{1,0:T(8,128)(2,1)}, u32[]{:S(2)}, u32[]{:S(2)}) collective-permute-start(bf16[960,512]{1,0:T(8,128)(2,1)S(1)} %broadcast_select_fusion), channel_id=1, source_target_pairs={{1,0},{2,3},{5,4},{6,7},{9,8},{10,11},{13,12},{14,15},{17,16},{18,... | collective-permute-start | bytes 2949128 | tf_op jit(solution)/shard_map/ppermute | solution.py:224
  138.2 40.2 %collective-permute-start.26 = (bf16[960,256]{1,0:T(8,128)(2,1)}, bf16[960,256]{1,0:T(8,128)(2,1)}, u32[]{:S(2)}, u32[]{:S(2)}) collective-permute-start(bf16[960,256]{1,0:T(8,128)(2,1)} %broadcast_select_fusion.1), channel_id=1, source_target_pairs={{1,0},{2,3},{5,4},{6,7},{9,8},{10,11},{13,12},{14,15},{17,16},{18,... | collective-permute-start | bytes 1474568 | tf_op jit(solution)/shard_map/ppermute | solution.py:224
  147.6 41.3 %collective-permute-start.18 = (bf16[960,256]{1,0:T(8,128)(2,1)S(1)}, bf16[960,256]{1,0:T(8,128)(2,1)}, u32[]{:S(2)}, u32[]{:S(2)}) collective-permute-start(bf16[960,256]{1,0:T(8,128)(2,1)S(1)} %broadcast_select_fusion.2), channel_id=1, source_target_pairs={{1,0},{2,3},{5,4},{6,7},{9,8},{10,11},{13,12},{14,15},{17,16},{18,... | collective-permute-start | bytes 1474568 | tf_op jit(solution)/shard_map/ppermute | solution.py:224
  185.3 22.8 %collective-permute-start.29 = (bf16[128,1024]{1,0:T(8,128)(2,1)}, bf16[128,1024]{1,0:T(8,128)(2,1)S(1)}, u32[]{:S(2)}, u32[]{:S(2)}) collective-permute-start(bf16[128,1024]{1,0:T(8,128)(2,1)} %get-tuple-element.40), channel_id=1, source_target_pairs={{0,24},{4,28},{8,16},{12,20},{16,8},{20,12},{24,0},{28,4},{1,25},{... | collective-permute-start | bytes 786440 | tf_op jit(solution)/shard_map/ppermute | solution.py:243
  187.1 22.5 %collective-permute-start.28 = (bf16[128,1024]{1,0:T(8,128)(2,1)}, bf16[128,1024]{1,0:T(8,128)(2,1)S(1)}, u32[]{:S(2)}, u32[]{:S(2)}) collective-permute-start(bf16[128,1024]{1,0:T(8,128)(2,1)} %get-tuple-element.39), channel_id=1, source_target_pairs={{0,16},{4,20},{8,24},{12,28},{16,0},{20,4},{24,8},{28,12},{1,17},{... | collective-permute-start | bytes 786440 | tf_op jit(solution)/shard_map/ppermute | solution.py:243
  188.3 22.1 %collective-permute-start.27 = (bf16[128,1024]{1,0:T(8,128)(2,1)}, bf16[128,1024]{1,0:T(8,128)(2,1)S(1)}, u32[]{:S(2)}, u32[]{:S(2)}) collective-permute-start(bf16[128,1024]{1,0:T(8,128)(2,1)} %get-tuple-element.38), channel_id=1, source_target_pairs={{0,8},{4,12},{8,0},{12,4},{16,24},{20,28},{24,16},{28,20},{1,9},{5... | collective-permute-start | bytes 786440 | tf_op jit(solution)/shard_map/ppermute | solution.py:243
  206.9 28.5 %collective-permute-start.13 = (bf16[256,1024]{1,0:T(8,128)(2,1)}, bf16[256,1024]{1,0:T(8,128)(2,1)S(1)}, u32[]{:S(2)}, u32[]{:S(2)}) collective-permute-start(bf16[256,1024]{1,0:T(8,128)(2,1)} %get-tuple-element.32), channel_id=1, source_target_pairs={{0,24},{4,28},{8,16},{12,20},{16,8},{20,12},{24,0},{28,4},{1,25},{... | collective-permute-start | bytes 1572872 | tf_op jit(solution)/shard_map/ppermute | solution.py:243
  208.1 27.3 %collective-permute-start.12 = (bf16[256,1024]{1,0:T(8,128)(2,1)}, bf16[256,1024]{1,0:T(8,128)(2,1)S(1)}, u32[]{:S(2)}, u32[]{:S(2)}) collective-permute-start(bf16[256,1024]{1,0:T(8,128)(2,1)} %get-tuple-element.31), channel_id=1, source_target_pairs={{0,16},{4,20},{8,24},{12,28},{16,0},{20,4},{24,8},{28,12},{1,17},{... | collective-permute-start | bytes 1572872 | tf_op jit(solution)/shard_map/ppermute | solution.py:243
  209.6 25.8 %collective-permute-start.11 = (bf16[256,1024]{1,0:T(8,128)(2,1)}, bf16[256,1024]{1,0:T(8,128)(2,1)S(1)}, u32[]{:S(2)}, u32[]{:S(2)}) collective-permute-start(bf16[256,1024]{1,0:T(8,128)(2,1)} %get-tuple-element.30), channel_id=1, source_target_pairs={{0,8},{4,12},{8,0},{12,4},{16,24},{20,28},{24,16},{28,20},{1,9},{5... | collective-permute-start | bytes 1572872 | tf_op jit(solution)/shard_map/ppermute | solution.py:243
  210.4 24.8 %collective-permute-start.20 = (bf16[128,1024]{1,0:T(8,128)(2,1)S(1)}, bf16[128,1024]{1,0:T(8,128)(2,1)S(1)}, u32[]{:S(2)}, u32[]{:S(2)}) collective-permute-start(bf16[128,1024]{1,0:T(8,128)(2,1)S(1)} %copy-done.17), channel_id=1, source_target_pairs={{0,16},{4,20},{8,24},{12,28},{16,0},{20,4},{24,8},{28,12},{1,17},{... | collective-permute-start | bytes 786440 | tf_op jit(solution)/shard_map/ppermute | solution.py:243
  211.7 23.6 %collective-permute-start.19 = (bf16[128,1024]{1,0:T(8,128)(2,1)S(1)}, bf16[128,1024]{1,0:T(8,128)(2,1)S(1)}, u32[]{:S(2)}, u32[]{:S(2)}) collective-permute-start(bf16[128,1024]{1,0:T(8,128)(2,1)S(1)} %copy-done.16), channel_id=1, source_target_pairs={{0,8},{4,12},{8,0},{12,4},{16,24},{20,28},{24,16},{28,20},{1,9},{5... | collective-permute-start | bytes 786440 | tf_op jit(solution)/shard_map/ppermute | solution.py:243
  (24 other events, 499.7 us)

commit v2 on v1

--- a/solution.py
+++ b/solution.py
@@ -127,49 +127,51 @@
     return table, where_of
 
 
-def products_kernel(n_stream, choice, kept, kept_pair, *refs):
-    streams, outs = refs[:n_stream], refs[n_stream : n_stream + len(refs) - n_stream - 2]
-    buffer, sems = refs[-2], refs[-1]
+def products_kernel(candidates, choice, kept, kept_pair, *refs):
+    n_ref = 1 + max(ref for ref, _, _ in candidates)
+    streams, outs = refs[:n_ref], refs[n_ref:-2]
+    buffer, sem = refs[-2], refs[-1]
     width = outs[0].shape[0]
-
-    def fetch(step):
-        for which in range(n_stream):
+    half = width * len(outs)
+
+    def pull(ref, offset, place):
+        return pltpu.make_async_copy(
+            streams[ref].at[:, pl.ds(offset, width)], buffer.at[:, pl.ds(place, width)], sem
+        )
+
+    for step in range(len(outs)):
+        for which, (ref, own, pair) in enumerate(candidates):
 
             @pl.when(choice[step] == which)
             def _():
-                pltpu.make_async_copy(
-                    streams[which], buffer.at[step % 2], sems.at[step % 2]
-                ).start()
-
-    fetch(0)
+                pull(ref, own, step * width).start()
+                pull(ref, pair, half + step * width).start()
+
+    for step in range(2 * len(outs)):
+        pull(0, 0, step * width).wait()
+    dims = (((0,), (0,)), ((), ()))
+    total = lax.dot_general(
+        buffer[:, :half], kept[...], dims, preferred_element_type=jnp.float32
+    ) + lax.dot_general(
+        buffer[:, half:], kept_pair[...], dims, preferred_element_type=jnp.float32
+    )
     for step, out in enumerate(outs):
-        if step + 1 < len(outs):
-            fetch(step + 1)
-        pltpu.make_async_copy(streams[0], buffer.at[step % 2], sems.at[step % 2]).wait()
-        dims = (((0,), (0,)), ((), ()))
-        total = lax.dot_general(
-            buffer[step % 2, :, :width], kept[...], dims, preferred_element_type=jnp.float32
-        )
-        total += lax.dot_general(
-            buffer[step % 2, :, width:], kept_pair[...], dims, preferred_element_type=jnp.float32
-        )
-        out[...] = total.astype(out.dtype)
-
-
-def products(choice, kept, kept_pair, streams, n_out):
-    rows, both = streams[0].shape
-    width, columns = both // 2, kept.shape[1]
+        out[...] = total[step * width : (step + 1) * width].astype(out.dtype)
+
+
+def products(choice, kept, kept_pair, streams, candidates, n_out, width):
+    rows, columns = kept.shape
     vmem = pl.BlockSpec(memory_space=pltpu.VMEM)
-    flops = n_out * 2 * both * rows * columns
+    flops = n_out * 4 * width * rows * columns
     return pl.pallas_call(
-        functools.partial(products_kernel, len(streams)),
+        functools.partial(products_kernel, candidates),
         in_specs=[pl.BlockSpec(memory_space=pltpu.SMEM), vmem, vmem]
         + [pl.BlockSpec(memory_space=pl.ANY)] * len(streams),
         out_specs=[vmem] * n_out,
         out_shape=[jax.ShapeDtypeStruct((width, columns), jnp.bfloat16)] * n_out,
         scratch_shapes=[
-            pltpu.VMEM((2, rows, both), jnp.bfloat16),
-            pltpu.SemaphoreType.DMA((2,)),
+            pltpu.VMEM((rows, 2 * n_out * width), jnp.bfloat16),
+            pltpu.SemaphoreType.DMA,
         ],
         cost_estimate=pl.CostEstimate(flops=flops, bytes_accessed=flops // 512, transcendentals=0),
         name="products",
@@ -187,6 +189,7 @@
     half = coeffs.shape[1] // 2
     widths = (half // 2, half // 4, half // 4)
     n_piece = len(widths)
+    last = n_col - 1
 
     bounds = lax.dynamic_slice_in_dim(offsets, own_row * per_dev, per_dev + 1)
     lengths = bounds[1:] - bounds[:-1]
@@ -220,28 +223,61 @@
     far_left = [lax.ppermute(unit, "col", right[1:]) for unit in from_left]
     far_right = [lax.ppermute(unit, "col", left[:-1]) for unit in from_right]
     on_left = own_col < n_col // 2
-    third = [
-        lax.ppermute(jnp.where(on_left, r, l), "col", [(1, 0), (n_col - 2, n_col - 1)])
-        for l, r in zip(far_left, far_right)
-    ]
+    helped = lax.ppermute(kept, "col", [(0, 1), (last, last - 1)])
+    helped_pair = lax.ppermute(helped, "row", swap)
 
     goals = chip ^ jnp.arange(n_chip, dtype=jnp.int32)
     gap = goals - own_col
-    choice = jnp.full((n_chip,), 5, jnp.int32)
-    for value, which in ((0, 0), (-1, 1), (1, 2), (-2, 3), (2, 4)):
+    choice = jnp.zeros((n_chip,), jnp.int32)
+    for value, which in ((-1, 1), (1, 2), (-2, 3), (2, 4)):
         choice = jnp.where(gap == value, which, choice)
-    rows = []
-    for which in range(n_piece):
+    totals = []
+    for which, width in enumerate(widths):
         streams = [
-            group_of[which]
-            for group_of in (units, from_left, from_right, far_left, far_right, third)
+            group_of[which] for group_of in (units, from_left, from_right, far_left, far_right)
         ]
-        parts = products(choice, kept, kept_pair, streams, n_chip)
+        candidates = tuple((ref, 0, width) for ref in range(len(streams)))
+        parts = products(choice, kept, kept_pair, streams, candidates, n_chip, width)
         total = parts[0].astype(jnp.float32)
         for d in range(1, n_chip):
             perm = [(r, r ^ (2 * d)) for r in range(n_row)]
             total = total + lax.ppermute(parts[d], "row", perm).astype(jnp.float32)
-        rows.append(total.astype(jnp.bfloat16))
+        totals.append(total)
+
+    quarter = half // n_chip
+    candidates = []
+    for q in range(n_chip):
+        begin, piece = q * quarter, 0
+        while begin >= widths[piece]:
+            begin, piece = begin - widths[piece], piece + 1
+        for side in range(2):
+            candidates.append((side * n_piece + piece, begin, widths[piece] + begin))
+    choice = 2 * goals + on_left.astype(jnp.int32)
+    parts = products(
+        choice, helped, helped_pair, far_left + far_right, tuple(candidates), n_chip, quarter
+    )
+    total = parts[0].astype(jnp.float32)
+    for d in range(1, n_chip):
+        perm = [(r, r ^ (2 * d)) for r in range(n_row)]
+        total = total + lax.ppermute(parts[d], "row", perm).astype(jnp.float32)
+    total = total.astype(jnp.bfloat16)
+    given = []
+    for d in range(n_chip):
+        perm = [
+            (((p ^ d) * 2 + s) * n_col + source, (p * 2 + s) * n_col + goal)
+            for source, goal, p in ((1, 0, last), (last - 1, last, 0))
+            for s in range(2)
+        ]
+        given.append(lax.ppermute(total, ("row", "col"), perm))
+    is_helped = ((own_col == 0) & (chip == last)) | ((own_col == last) & (chip == 0))
+    rows, begin = [], 0
+    for total, width in zip(totals, widths):
+        gifts = [
+            jnp.where(on_left, given[q ^ last], given[q])
+            for q in range(begin // quarter, (begin + width) // quarter)
+        ]
+        rows.append(jnp.where(is_helped, jnp.concatenate(gifts), total.astype(jnp.bfloat16)))
+        begin += width
     return jnp.concatenate(rows, axis=0)
 
 

time: 238 us -> 271 us (1.14)
  the two profiles are of different devices: /device:TPU:0 before, /device:TPU:24 now
where the time goes in v2:
time: 271 us; the launch traced here: 270 us
  waiting for transfers between devices  163 us (60%)
  starting transfers between devices  49.9 us (18%)
  Pallas kernels  43.8 us (16%)
  other arithmetic  8.71 us (3%)
  local copies, waits for them, and re-layouts  3.96 us (1%)
    ppermute x3, waiting for transfers between devices, line_body(): far_left = [lax.ppermute(unit, 'col', right[1:]) for unit in from_left]  63.7 us
    ppermute x3, waiting for transfers between devices, line_body(): from_right = [lax.ppermute(unit, 'col', left) for unit in units]  47.1 us
    pallas_call x4, Pallas kernels, products(): pl.pallas_call(functools.partial(products_kernel, candidates), in_specs=[...  31.1 us
    ppermute x3, waiting for transfers between devices, line_body(): lax.ppermute(outgoing[d], 'row', [(r, r ^ 2 * d) for r in range(n_row)])  27.4 us
    ppermute x12, waiting for transfers between devices, line_body(): total = total + lax.ppermute(parts[d], 'row', perm).astype(jnp.float32)  16.5 us
    ppermute x12, starting transfers between devices, line_body(): total = total + lax.ppermute(parts[d], 'row', perm).astype(jnp.float32)  12.6 us
    ppermute x3, starting transfers between devices, line_body(): from_right = [lax.ppermute(unit, 'col', left) for unit in units]  12.2 us
    ppermute x4, waiting for transfers between devices, line_body(): given.append(lax.ppermute(total, ('row', 'col'), perm))  8.57 us
  transfers between devices with their start and end apart: 36, of which 10 were waited for; matrix products, arithmetic and copies ran while one was open for 2% of the time, Pallas kernels for 15%

profile of v2, /device:TPU:24, one launch (start us, length us, event | category | flops | bytes accessed | tf_op | source)
XLA Modules:
  0.0 270.3 jit_solution(14668083208267234980)
XLA Ops:
  2.6 3.4 %sort_blocks.1 = (bf16[10,32,1024]{2,1,0:T(8,128)(2,1)}, bf16[10,32,1024]{2,1,0:T(8,128)(2,1)}, bf16[10,32,1024]{2,1,0:T(8,128)(2,1)}, bf16[10,32,1024]{2,1,0:T(8,128)(2,1)}) custom-call(s32[40]{0:T(128)} %select_reduce_fusion.1.table, bf16[40,32,1024]{2,1,0:T(8,128)(2,1)} %blocks.1), custom_call_target="tpu_custom_call" | custom-call | tf_op jit(solution)/shard_map/sort_blocks/pallas_call | solution.py:68
  7.5 1.5 collective-permute-start.1
  10.5 13.3 %collective-permute-done.refs_1_ = bf16[10,32,1024]{2,1,0:T(8,128)(2,1)S(1)} collective-permute-done((bf16[10,32,1024]{2,1,0:T(8,128)(2,1)}, bf16[10,32,1024]{2,1,0:T(8,128)(2,1)S(1)}, u32[]{:S(2)}, u32[]{:S(2)}) %collective-permute-start) | collective-permute-done | bytes 655392 | tf_op jit(solution)/shard_map/ppermute | solution.py:215
  23.9 14.1 %collective-permute-done.1.refs_2_ = bf16[10,32,1024]{2,1,0:T(8,128)(2,1)S(1)} collective-permute-done((bf16[10,32,1024]{2,1,0:T(8,128)(2,1)}, bf16[10,32,1024]{2,1,0:T(8,128)(2,1)S(1)}, u32[]{:S(2)}, u32[]{:S(2)}) %collective-permute-start.1) | collective-permute-done | bytes 655392 | tf_op jit(solution)/shard_map/ppermute | solution.py:215
  40.9 4.9 %pack_coeffs.1 = (bf16[960,512]{1,0:T(8,128)(2,1)}, bf16[960,512]{1,0:T(8,128)(2,1)}) custom-call(s32[40]{0:T(128)} %slice_subtract_fusion.lengths, s32[1]{0:T(128)} %bitcast.2.core, bf16[1280,1024]{1,0:T(8,128)(2,1)} %coeffs.1), custom_call_target="tpu_custom_call" | custom-call | tf_op jit(solution)/shard_map/pack_coeffs/pallas_call | solution.py:49
  48.8 4.3 %pack_kept.1.kept = bf16[960,1024]{1,0:T(8,128)(2,1)} custom-call(s32[40]{0:T(128)} %select_reduce_fusion.where_of, s32[40]{0:T(128)} %slice_subtract_fusion.lengths, s32[40]{0:T(128)} %dynamic-slice_bitcast_fusion.alive, bf16[10,32,1024]{2,1,0:T(8,128)(2,1)} %get-tuple-element.27.refs_0_, bf16[10,32,1024]{2,1,0:T(8,128)(2,1)} %copy-done.2, ...), custom_call_target="tpu_custom_call" | custom-call | tf_op jit(solution)/shard_map/pack_kept/pallas_call | solution.py:98
  53.1 3.7 %collective-permute-start.4 = (bf16[960,1024]{1,0:T(8,128)(2,1)}, bf16[960,1024]{1,0:T(8,128)(2,1)}, u32[]{:S(2)}, u32[]{:S(2)}) collective-permute-start(bf16[960,1024]{1,0:T(8,128)(2,1)} %pack_kept.1.kept), channel_id=1, source_target_pairs={{0,1},{3,2},{4,5},{7,6},{8,9},{11,10},{12,13},{15,14},{16,17},{19,... | collective-permute-start | bytes 5898248 | tf_op jit(solution)/shard_map/ppermute | solution.py:226
  59.8 4.7 %collective-permute-start.15 = (bf16[960,256]{1,0:T(8,128)(2,1)S(1)}, bf16[960,256]{1,0:T(8,128)(2,1)S(1)}, u32[]{:S(2)}, u32[]{:S(2)}) collective-permute-start(bf16[960,256]{1,0:T(8,128)(2,1)S(1)} %pad_maximum_fusion.3.refs_0_), channel_id=1, source_target_pairs={{1,0},{2,1},{3,2},{5,4},{6,5},{7,6},{9,8},{10,9},{11,10},{13,12},{... | collective-permute-start | bytes 1474568 | tf_op jit(solution)/shard_map/ppermute | solution.py:209
  65.9 43.5 %collective-permute-done.17.refs_2_ = bf16[960,256]{1,0:T(8,128)(2,1)S(1)} collective-permute-done((bf16[960,256]{1,0:T(8,128)(2,1)S(1)}, bf16[960,256]{1,0:T(8,128)(2,1)S(1)}, u32[]{:S(2)}, u32[]{:S(2)}) %collective-permute-start.17) | collective-permute-done | bytes 491552 | tf_op jit(solution)/shard_map/ppermute | solution.py:209
  110.2 6.1 %collective-permute-start.13 = (bf16[960,512]{1,0:T(8,128)(2,1)S(1)}, bf16[960,512]{1,0:T(8,128)(2,1)}, u32[]{:S(2)}, u32[]{:S(2)}) collective-permute-start(bf16[960,512]{1,0:T(8,128)(2,1)S(1)} %pad_maximum_fusion.2.refs_0_), channel_id=1, source_target_pairs={{1,0},{2,1},{3,2},{5,4},{6,5},{7,6},{9,8},{10,9},{11,10},{13,12},{... | collective-permute-start | bytes 2949128 | tf_op jit(solution)/shard_map/ppermute | solution.py:209
  116.3 3.6 %collective-permute-done.15.refs_2_ = bf16[960,256]{1,0:T(8,128)(2,1)S(1)} collective-permute-done((bf16[960,256]{1,0:T(8,128)(2,1)S(1)}, bf16[960,256]{1,0:T(8,128)(2,1)S(1)}, u32[]{:S(2)}, u32[]{:S(2)}) %collective-permute-start.15) | collective-permute-done | bytes 491552 | tf_op jit(solution)/shard_map/ppermute | solution.py:209
  123.1 31.9 %collective-permute-done.12.refs_2_.refs_3_ = bf16[960,256]{1,0:T(8,128)(2,1)S(1)} collective-permute-done((bf16[960,256]{1,0:T(8,128)(2,1)S(1)}, bf16[960,256]{1,0:T(8,128)(2,1)S(1)}, u32[]{:S(2)}, u32[]{:S(2)}) %collective-permute-start.12) | collective-permute-done | bytes 491552 | tf_op jit(solution)/shard_map/ppermute | solution.py:223
  156.4 1.6 collective-permute-start.14
  161.3 31.8 %collective-permute-done.10.refs_1_.refs_3_ = bf16[960,256]{1,0:T(8,128)(2,1)} collective-permute-done((bf16[960,256]{1,0:T(8,128)(2,1)}, bf16[960,256]{1,0:T(8,128)(2,1)}, u32[]{:S(2)}, u32[]{:S(2)}) %collective-permute-start.10) | collective-permute-done | bytes 491552 | tf_op jit(solution)/shard_map/ppermute | solution.py:223
  193.1 7.1 %products.4 = (bf16[128,1024]{1,0:T(8,128)(2,1)}, bf16[128,1024]{1,0:T(8,128)(2,1)}, bf16[128,1024]{1,0:T(8,128)(2,1)}, bf16[128,1024]{1,0:T(8,128)(2,1)}) custom-call(s32[4]{0:T(128)} %multiply_add_fusion.choice, bf16[960,1024]{1,0:T(8,128)(2,1)} %collective-permute-done.4.kept, bf16[960,1024]{1,0:T(8,128)(2,1)} %collective-permute-done.5.kept_pair, ...), custom_call_target="tpu_custom_call" | custom-call | flops 2013265920 | bytes 3932160 | tf_op jit(solution)/shard_map/products/pallas_call | solution.py:166
  204.3 7.1 %products.7 = (bf16[128,1024]{1,0:T(8,128)(2,1)}, bf16[128,1024]{1,0:T(8,128)(2,1)}, bf16[128,1024]{1,0:T(8,128)(2,1)}, bf16[128,1024]{1,0:T(8,128)(2,1)}) custom-call(s32[4]{0:T(128)} %compare_select_fusion.3.choice, bf16[960,1024]{1,0:T(8,128)(2,1)} %pack_kept.1.kept, bf16[960,1024]{1,0:T(8,128)(2,1)} %collective-permute-done.26.kept_pair, ...), custom_call_target="tpu_custom_call" | custom-call | flops 2013265920 | bytes 3932160 | tf_op jit(solution)/shard_map/products/pallas_call | solution.py:166
  215.0 7.0 %products.6 = (bf16[128,1024]{1,0:T(8,128)(2,1)}, bf16[128,1024]{1,0:T(8,128)(2,1)}, bf16[128,1024]{1,0:T(8,128)(2,1)}, bf16[128,1024]{1,0:T(8,128)(2,1)}) custom-call(s32[4]{0:T(128)} %compare_select_fusion.3.choice, bf16[960,1024]{1,0:T(8,128)(2,1)} %pack_kept.1.kept, bf16[960,1024]{1,0:T(8,128)(2,1)} %collective-permute-done.26.kept_pair, ...), custom_call_target="tpu_custom_call" | custom-call | flops 2013265920 | bytes 3932160 | tf_op jit(solution)/shard_map/products/pallas_call | solution.py:166
  224.3 1.5 collective-permute-start.32
  228.6 9.9 %products.5 = (bf16[256,1024]{1,0:T(8,128)(2,1)}, bf16[256,1024]{1,0:T(8,128)(2,1)}, bf16[256,1024]{1,0:T(8,128)(2,1)}, bf16[256,1024]{1,0:T(8,128)(2,1)}) custom-call(s32[4]{0:T(128)} %compare_select_fusion.3.choice, bf16[960,1024]{1,0:T(8,128)(2,1)} %pack_kept.1.kept, bf16[960,1024]{1,0:T(8,128)(2,1)} %collective-permute-done.26.kept_pair, ...), custom_call_target="tpu_custom_call" | custom-call | flops 4026531840 | bytes 7864320 | tf_op jit(solution)/shard_map/products/pallas_call | solution.py:166
  238.7 1.6 collective-permute-done.31
  240.3 1.8 collective-permute-start.29
  245.1 5.4 %collective-permute-done.23 = bf16[128,1024]{1,0:T(8,128)(2,1)S(1)} collective-permute-done((bf16[128,1024]{1,0:T(8,128)(2,1)S(1)}, bf16[128,1024]{1,0:T(8,128)(2,1)S(1)}, u32[]{:S(2)}, u32[]{:S(2)}) %collective-permute-start.23) | collective-permute-done | bytes 262176 | tf_op jit(solution)/shard_map/ppermute | solution.py:271
  250.4 3.2 %collective-permute-done.22 = bf16[128,1024]{1,0:T(8,128)(2,1)S(1)} collective-permute-done((bf16[128,1024]{1,0:T(8,128)(2,1)S(1)}, bf16[128,1024]{1,0:T(8,128)(2,1)S(1)}, u32[]{:S(2)}, u32[]{:S(2)}) %collective-permute-start.22) | collective-permute-done | bytes 262176 | tf_op jit(solution)/shard_map/ppermute | solution.py:271
  253.9 14.8 %collective-permute-done.28 = bf16[256,1024]{1,0:T(8,128)(2,1)S(1)} collective-permute-done((bf16[256,1024]{1,0:T(8,128)(2,1)}, bf16[256,1024]{1,0:T(8,128)(2,1)S(1)}, u32[]{:S(2)}, u32[]{:S(2)}) %collective-permute-start.28) | collective-permute-done | bytes 524320 | tf_op jit(solution)/shard_map/ppermute | solution.py:244
  (130 shorter events, 41.7 us)
Async XLA Ops:
  6.0 17.8 %collective-permute-start = (bf16[10,32,1024]{2,1,0:T(8,128)(2,1)}, bf16[10,32,1024]{2,1,0:T(8,128)(2,1)S(1)}, u32[]{:S(2)}, u32[]{:S(2)}) collective-permute-start(bf16[10,32,1024]{2,1,0:T(8,128)(2,1)} %get-tuple-element.28), channel_id=1, source_target_pairs={{0,8},{4,12},{8,0},{12,4},{16,24},{20,28},{24,16},{28,20},{1,9},{5... | collective-permute-start | bytes 1966088 | tf_op jit(solution)/shard_map/ppermute | solution.py:215
  7.5 30.4 %collective-permute-start.1 = (bf16[10,32,1024]{2,1,0:T(8,128)(2,1)}, bf16[10,32,1024]{2,1,0:T(8,128)(2,1)S(1)}, u32[]{:S(2)}, u32[]{:S(2)}) collective-permute-start(bf16[10,32,1024]{2,1,0:T(8,128)(2,1)} %get-tuple-element.29), channel_id=1, source_target_pairs={{0,16},{4,20},{8,24},{12,28},{16,0},{20,4},{24,8},{28,12},{1,17},{... | collective-permute-start | bytes 1966088 | tf_op jit(solution)/shard_map/ppermute | solution.py:215
  9.0 29.0 %collective-permute-start.2 = (bf16[10,32,1024]{2,1,0:T(8,128)(2,1)}, bf16[10,32,1024]{2,1,0:T(8,128)(2,1)S(1)}, u32[]{:S(2)}, u32[]{:S(2)}) collective-permute-start(bf16[10,32,1024]{2,1,0:T(8,128)(2,1)} %get-tuple-element.30), channel_id=1, source_target_pairs={{0,24},{4,28},{8,16},{12,20},{16,8},{20,12},{24,0},{28,4},{1,25},{... | collective-permute-start | bytes 1966088 | tf_op jit(solution)/shard_map/ppermute | solution.py:215
  53.1 68.1 %collective-permute-start.4 = (bf16[960,1024]{1,0:T(8,128)(2,1)}, bf16[960,1024]{1,0:T(8,128)(2,1)}, u32[]{:S(2)}, u32[]{:S(2)}) collective-permute-start(bf16[960,1024]{1,0:T(8,128)(2,1)} %pack_kept.1.kept), channel_id=1, source_target_pairs={{0,1},{3,2},{4,5},{7,6},{8,9},{11,10},{12,13},{15,14},{16,17},{19,... | collective-permute-start | bytes 5898248 | tf_op jit(solution)/shard_map/ppermute | solution.py:226
  57.0 52.4 %collective-permute-start.17 = (bf16[960,256]{1,0:T(8,128)(2,1)S(1)}, bf16[960,256]{1,0:T(8,128)(2,1)S(1)}, u32[]{:S(2)}, u32[]{:S(2)}) collective-permute-start(bf16[960,256]{1,0:T(8,128)(2,1)S(1)} %pad_maximum_fusion.4.refs_0_), channel_id=1, source_target_pairs={{1,0},{2,1},{3,2},{5,4},{6,5},{7,6},{9,8},{10,9},{11,10},{13,12},{... | collective-permute-start | bytes 1474568 | tf_op jit(solution)/shard_map/ppermute | solution.py:209
  58.4 51.8 %collective-permute-start.11 = (bf16[960,256]{1,0:T(8,128)(2,1)S(1)}, bf16[960,256]{1,0:T(8,128)(2,1)S(1)}, u32[]{:S(2)}, u32[]{:S(2)}) collective-permute-start(bf16[960,256]{1,0:T(8,128)(2,1)S(1)} %pad_maximum_fusion.4.refs_0_), channel_id=1, source_target_pairs={{0,1},{1,2},{2,3},{4,5},{5,6},{6,7},{8,9},{9,10},{10,11},{12,13},{... | collective-permute-start | bytes 1474568 | tf_op jit(solution)/shard_map/ppermute | solution.py:208
  59.8 60.1 %collective-permute-start.15 = (bf16[960,256]{1,0:T(8,128)(2,1)S(1)}, bf16[960,256]{1,0:T(8,128)(2,1)S(1)}, u32[]{:S(2)}, u32[]{:S(2)}) collective-permute-start(bf16[960,256]{1,0:T(8,128)(2,1)S(1)} %pad_maximum_fusion.3.refs_0_), channel_id=1, source_target_pairs={{1,0},{2,1},{3,2},{5,4},{6,5},{7,6},{9,8},{10,9},{11,10},{13,12},{... | collective-permute-start | bytes 1474568 | tf_op jit(solution)/shard_map/ppermute | solution.py:209
  64.5 56.8 %collective-permute-start.9 = (bf16[960,256]{1,0:T(8,128)(2,1)S(1)}, bf16[960,256]{1,0:T(8,128)(2,1)}, u32[]{:S(2)}, u32[]{:S(2)}) collective-permute-start(bf16[960,256]{1,0:T(8,128)(2,1)S(1)} %pad_maximum_fusion.3.refs_0_), channel_id=1, source_target_pairs={{0,1},{1,2},{2,3},{4,5},{5,6},{6,7},{8,9},{9,10},{10,11},{12,13},{... | collective-permute-start | bytes 1474568 | tf_op jit(solution)/shard_map/ppermute | solution.py:208
  110.2 46.2 %collective-permute-start.13 = (bf16[960,512]{1,0:T(8,128)(2,1)S(1)}, bf16[960,512]{1,0:T(8,128)(2,1)}, u32[]{:S(2)}, u32[]{:S(2)}) collective-permute-start(bf16[960,512]{1,0:T(8,128)(2,1)S(1)} %pad_maximum_fusion.2.refs_0_), channel_id=1, source_target_pairs={{1,0},{2,1},{3,2},{5,4},{6,5},{7,6},{9,8},{10,9},{11,10},{13,12},{... | collective-permute-start | bytes 2949128 | tf_op jit(solution)/shard_map/ppermute | solution.py:209
  120.0 38.1 %collective-permute-start.7 = (bf16[960,512]{1,0:T(8,128)(2,1)S(1)}, bf16[960,512]{1,0:T(8,128)(2,1)}, u32[]{:S(2)}, u32[]{:S(2)}) collective-permute-start(bf16[960,512]{1,0:T(8,128)(2,1)S(1)} %pad_maximum_fusion.2.refs_0_), channel_id=1, source_target_pairs={{0,1},{1,2},{2,3},{4,5},{5,6},{6,7},{8,9},{9,10},{10,11},{12,13},{... | collective-permute-start | bytes 2949128 | tf_op jit(solution)/shard_map/ppermute | solution.py:208
  121.3 71.9 %collective-permute-start.5 = (bf16[960,1024]{1,0:T(8,128)(2,1)}, bf16[960,1024]{1,0:T(8,128)(2,1)}, u32[]{:S(2)}, u32[]{:S(2)}) collective-permute-start(bf16[960,1024]{1,0:T(8,128)(2,1)} %collective-permute-done.4.kept), channel_id=1, source_target_pairs={{0,4},{4,0},{8,12},{12,8},{16,20},{20,16},{24,28},{28,24},{1,5},{5... | collective-permute-start | bytes 5898248 | tf_op jit(solution)/shard_map/ppermute | solution.py:227
  121.4 82.9 %collective-permute-start.26 = (bf16[960,1024]{1,0:T(8,128)(2,1)S(1)}, bf16[960,1024]{1,0:T(8,128)(2,1)}, u32[]{:S(2)}, u32[]{:S(2)}) collective-permute-start(bf16[960,1024]{1,0:T(8,128)(2,1)S(1)} %copy-done.1), channel_id=1, source_target_pairs={{0,4},{4,0},{8,12},{12,8},{16,20},{20,16},{24,28},{28,24},{1,5},{5... | collective-permute-start | bytes 5898248 | tf_op jit(solution)/shard_map/ppermute | solution.py:221
  121.8 33.2 %collective-permute-start.12 = (bf16[960,256]{1,0:T(8,128)(2,1)S(1)}, bf16[960,256]{1,0:T(8,128)(2,1)S(1)}, u32[]{:S(2)}, u32[]{:S(2)}) collective-permute-start(bf16[960,256]{1,0:T(8,128)(2,1)S(1)} %collective-permute-done.11.refs_1_), channel_id=1, source_target_pairs={{1,2},{2,3},{5,6},{6,7},{9,10},{10,11},{13,14},{14,15},{17,18},{18... | collective-permute-start | bytes 1474568 | tf_op jit(solution)/shard_map/ppermute | solution.py:223
  156.4 36.7 %collective-permute-start.14 = (bf16[960,512]{1,0:T(8,128)(2,1)}, bf16[960,512]{1,0:T(8,128)(2,1)}, u32[]{:S(2)}, u32[]{:S(2)}) collective-permute-start(bf16[960,512]{1,0:T(8,128)(2,1)} %collective-permute-done.13.refs_2_), channel_id=1, source_target_pairs={{1,0},{2,1},{5,4},{6,5},{9,8},{10,9},{13,12},{14,13},{17,16},{18,1... | collective-permute-start | bytes 2949128 | tf_op jit(solution)/shard_map/ppermute | solution.py:224
  158.1 35.0 %collective-permute-start.8 = (bf16[960,512]{1,0:T(8,128)(2,1)}, bf16[960,512]{1,0:T(8,128)(2,1)}, u32[]{:S(2)}, u32[]{:S(2)}) collective-permute-start(bf16[960,512]{1,0:T(8,128)(2,1)} %collective-permute-done.7.refs_1_), channel_id=1, source_target_pairs={{1,2},{2,3},{5,6},{6,7},{9,10},{10,11},{13,14},{14,15},{17,18},{18... | collective-permute-start | bytes 2949128 | tf_op jit(solution)/shard_map/ppermute | solution.py:223
  159.4 33.7 %collective-permute-start.10 = (bf16[960,256]{1,0:T(8,128)(2,1)}, bf16[960,256]{1,0:T(8,128)(2,1)}, u32[]{:S(2)}, u32[]{:S(2)}) collective-permute-start(bf16[960,256]{1,0:T(8,128)(2,1)} %collective-permute-done.9.refs_1_), channel_id=1, source_target_pairs={{1,2},{2,3},{5,6},{6,7},{9,10},{10,11},{13,14},{14,15},{17,18},{18... | collective-permute-start | bytes 1474568 | tf_op jit(solution)/shard_map/ppermute | solution.py:223
  201.8 20.2 %collective-permute-start.20 = (bf16[128,1024]{1,0:T(8,128)(2,1)}, bf16[128,1024]{1,0:T(8,128)(2,1)S(1)}, u32[]{:S(2)}, u32[]{:S(2)}) collective-permute-start(bf16[128,1024]{1,0:T(8,128)(2,1)} %get-tuple-element.35), channel_id=1, source_target_pairs={{0,16},{4,20},{8,24},{12,28},{16,0},{20,4},{24,8},{28,12},{1,17},{... | collective-permute-start | bytes 786440 | tf_op jit(solution)/shard_map/ppermute | solution.py:262
  202.8 20.3 %collective-permute-start.21 = (bf16[128,1024]{1,0:T(8,128)(2,1)}, bf16[128,1024]{1,0:T(8,128)(2,1)S(1)}, u32[]{:S(2)}, u32[]{:S(2)}) collective-permute-start(bf16[128,1024]{1,0:T(8,128)(2,1)} %get-tuple-element.36), channel_id=1, source_target_pairs={{0,24},{4,28},{8,16},{12,20},{16,8},{20,12},{24,0},{28,4},{1,25},{... | collective-permute-start | bytes 786440 | tf_op jit(solution)/shard_map/ppermute | solution.py:262
  222.0 16.6 %collective-permute-start.30 = (bf16[128,1024]{1,0:T(8,128)(2,1)}, bf16[128,1024]{1,0:T(8,128)(2,1)S(1)}, u32[]{:S(2)}, u32[]{:S(2)}) collective-permute-start(bf16[128,1024]{1,0:T(8,128)(2,1)} %get-tuple-element.42), channel_id=1, source_target_pairs={{0,8},{4,12},{8,0},{12,4},{16,24},{20,28},{24,16},{28,20},{1,9},{5... | collective-permute-start | bytes 786440 | tf_op jit(solution)/shard_map/ppermute | solution.py:244
  223.1 17.2 %collective-permute-start.31 = (bf16[128,1024]{1,0:T(8,128)(2,1)}, bf16[128,1024]{1,0:T(8,128)(2,1)S(1)}, u32[]{:S(2)}, u32[]{:S(2)}) collective-permute-start(bf16[128,1024]{1,0:T(8,128)(2,1)} %get-tuple-element.43), channel_id=1, source_target_pairs={{0,16},{4,20},{8,24},{12,28},{16,0},{20,4},{24,8},{28,12},{1,17},{... | collective-permute-start | bytes 786440 | tf_op jit(solution)/shard_map/ppermute | solution.py:244
  225.8 16.3 %collective-permute-start.25 = (bf16[128,1024]{1,0:T(8,128)(2,1)S(1)}, bf16[128,1024]{1,0:T(8,128)(2,1)S(1)}, u32[]{:S(2)}, u32[]{:S(2)}) collective-permute-start(bf16[128,1024]{1,0:T(8,128)(2,1)S(1)} %add_convert_fusion.3), channel_id=1, source_target_pairs={{17,24},{21,28},{10,3},{14,7}} | collective-permute-start | bytes 786440 | tf_op jit(solution)/shard_map/ppermute | solution.py:271
  227.1 16.3 %collective-permute-start.24 = (bf16[128,1024]{1,0:T(8,128)(2,1)S(1)}, bf16[128,1024]{1,0:T(8,128)(2,1)S(1)}, u32[]{:S(2)}, u32[]{:S(2)}) collective-permute-start(bf16[128,1024]{1,0:T(8,128)(2,1)S(1)} %add_convert_fusion.3), channel_id=1, source_target_pairs={{9,24},{13,28},{18,3},{22,7}} | collective-permute-start | bytes 786440 | tf_op jit(solution)/shard_map/ppermute | solution.py:271
  240.3 28.4 %collective-permute-start.28 = (bf16[256,1024]{1,0:T(8,128)(2,1)}, bf16[256,1024]{1,0:T(8,128)(2,1)S(1)}, u32[]{:S(2)}, u32[]{:S(2)}) collective-permute-start(bf16[256,1024]{1,0:T(8,128)(2,1)} %get-tuple-element.39), channel_id=1, source_target_pairs={{0,16},{4,20},{8,24},{12,28},{16,0},{20,4},{24,8},{28,12},{1,17},{... | collective-permute-start | bytes 1572872 | tf_op jit(solution)/shard_map/ppermute | solution.py:244
  240.3 28.4 %collective-permute-start.29 = (bf16[256,1024]{1,0:T(8,128)(2,1)}, bf16[256,1024]{1,0:T(8,128)(2,1)S(1)}, u32[]{:S(2)}, u32[]{:S(2)}) collective-permute-start(bf16[256,1024]{1,0:T(8,128)(2,1)} %get-tuple-element.40), channel_id=1, source_target_pairs={{0,24},{4,28},{8,16},{12,20},{16,8},{20,12},{24,0},{28,4},{1,25},{... | collective-permute-start | bytes 1572872 | tf_op jit(solution)/shard_map/ppermute | solution.py:244
  (32 other events, 768.4 us)

commit v3 on v2

--- a/solution.py
+++ b/solution.py
@@ -27,33 +27,42 @@
     return (wanted == col).astype(jnp.bfloat16)
 
 
-def pack_coeffs_kernel(atom_w, group, widths, lengths, core, coeffs, *pieces):
+def pack_coeffs_kernel(atom_w, group, per_dev, widths, place, offsets, mine, paired, *pieces):
     step = pl.program_id(0)
-    first = [lengths[step * group + 2 * pair] for pair in range(group // 2)]
-    chooser = selector(first, None, atom_w, group)
-    half = sum(widths)
-    for side in range(2):
-        start = half * jnp.where(core[0] == side, 0, 1)
-        for which, width in enumerate(widths):
-            offset = pl.multiple_of(start + sum(widths[:which]), 128)
-            block = coeffs[:, pl.ds(offset, width)]
-            pieces[side * len(widths) + which][...] = jnp.dot(
-                chooser, block, preferred_element_type=jnp.float32
+    for side, block in enumerate((mine, paired)):
+        base = (place[0] if side == 0 else place[0] ^ 1) * per_dev + step * group
+        marks = [offsets[base + atom] for atom in range(group)]
+        first = [marks[2 * pair + 1] - marks[2 * pair] for pair in range(group // 2)]
+        chooser = selector(first, None, atom_w, group)
+        begin = 0
+        for piece, width in zip(pieces, widths):
+            piece[:, side * width : (side + 1) * width] = jnp.dot(
+                chooser, block[:, begin : begin + width], preferred_element_type=jnp.float32
             ).astype(jnp.bfloat16)
-
-
-def pack_coeffs(coeffs, lengths, core, per_dev, atom_w, group, widths):
+            begin += width
+
+
+def pack_coeffs(coeffs, paired, offsets, own_row, per_dev, atom_w, group, widths):
     rows_in, rows_out = group * atom_w, group // 2 * (3 * atom_w // 2)
-    steps = per_dev // group
-    smem = pl.BlockSpec(memory_space=pltpu.SMEM)
+    steps, half = per_dev // group, paired.shape[1]
     return pl.pallas_call(
-        functools.partial(pack_coeffs_kernel, atom_w, group, widths),
-        grid=(steps,),
-        in_specs=[smem, smem, pl.BlockSpec((rows_in, coeffs.shape[1]), lambda i: (i, 0))],
-        out_specs=[pl.BlockSpec((rows_out, w), lambda i: (i, 0)) for w in widths * 2],
-        out_shape=[jax.ShapeDtypeStruct((steps * rows_out, w), jnp.bfloat16) for w in widths * 2],
+        functools.partial(pack_coeffs_kernel, atom_w, group, per_dev, widths),
+        grid_spec=pltpu.PrefetchScalarGridSpec(
+            num_scalar_prefetch=2,
+            grid=(steps,),
+            in_specs=[
+                pl.BlockSpec((rows_in, half), lambda i, place, offsets: (i, place[0] % 2)),
+                pl.BlockSpec((rows_in, half), lambda i, place, offsets: (i, 0)),
+            ],
+            out_specs=[
+                pl.BlockSpec((rows_out, 2 * w), lambda i, place, offsets: (i, 0)) for w in widths
+            ],
+        ),
+        out_shape=[
+            jax.ShapeDtypeStruct((steps * rows_out, 2 * w), jnp.bfloat16) for w in widths
+        ],
         name="pack_coeffs",
-    )(lengths, core, coeffs)
+    )(own_row.astype(jnp.int32).reshape(1), offsets, coeffs, paired)
 
 
 def sort_blocks_kernel(slots, table, blocks, *outs):
@@ -129,32 +138,43 @@
 
 def products_kernel(candidates, choice, kept, kept_pair, *refs):
     n_ref = 1 + max(ref for ref, _, _ in candidates)
-    streams, outs = refs[:n_ref], refs[n_ref:-2]
-    buffer, sem = refs[-2], refs[-1]
+    streams, outs = refs[:n_ref], refs[n_ref:-3]
+    buffer, held, sems = refs[-3:]
     width = outs[0].shape[0]
     half = width * len(outs)
 
-    def pull(ref, offset, place):
+    def pull(side, ref, offset, place):
         return pltpu.make_async_copy(
-            streams[ref].at[:, pl.ds(offset, width)], buffer.at[:, pl.ds(place, width)], sem
+            streams[ref].at[:, pl.ds(offset, width)],
+            buffer.at[:, pl.ds(side * half + place, width)],
+            sems.at[side],
         )
 
-    for step in range(len(outs)):
-        for which, (ref, own, pair) in enumerate(candidates):
-
-            @pl.when(choice[step] == which)
-            def _():
-                pull(ref, own, step * width).start()
-                pull(ref, pair, half + step * width).start()
-
-    for step in range(2 * len(outs)):
-        pull(0, 0, step * width).wait()
-    dims = (((0,), (0,)), ((), ()))
-    total = lax.dot_general(
-        buffer[:, :half], kept[...], dims, preferred_element_type=jnp.float32
-    ) + lax.dot_general(
-        buffer[:, half:], kept_pair[...], dims, preferred_element_type=jnp.float32
-    )
+    loads = [
+        pltpu.make_async_copy(source, held.at[side], sems.at[2 + side])
+        for side, source in enumerate((kept, kept_pair))
+    ]
+    for side in range(2):
+        for step in range(len(outs)):
+            for which, (ref, *begin) in enumerate(candidates):
+
+                @pl.when(choice[step] == which)
+                def _():
+                    pull(side, ref, begin[side], step * width).start()
+
+        loads[side].start()
+    total = None
+    for side in range(2):
+        for step in range(len(outs)):
+            pull(side, 0, 0, step * width).wait()
+        loads[side].wait()
+        term = lax.dot_general(
+            buffer[:, side * half : (side + 1) * half],
+            held[side],
+            (((0,), (0,)), ((), ())),
+            preferred_element_type=jnp.float32,
+        )
+        total = term if total is None else total + term
     for step, out in enumerate(outs):
         out[...] = total[step * width : (step + 1) * width].astype(out.dtype)
 
@@ -165,13 +185,14 @@
     flops = n_out * 4 * width * rows * columns
     return pl.pallas_call(
         functools.partial(products_kernel, candidates),
-        in_specs=[pl.BlockSpec(memory_space=pltpu.SMEM), vmem, vmem]
-        + [pl.BlockSpec(memory_space=pl.ANY)] * len(streams),
+        in_specs=[pl.BlockSpec(memory_space=pltpu.SMEM)]
+        + [pl.BlockSpec(memory_space=pl.ANY)] * (2 + len(streams)),
         out_specs=[vmem] * n_out,
         out_shape=[jax.ShapeDtypeStruct((width, columns), jnp.bfloat16)] * n_out,
         scratch_shapes=[
             pltpu.VMEM((rows, 2 * n_out * width), jnp.bfloat16),
-            pltpu.SemaphoreType.DMA,
+            pltpu.VMEM((2, rows, columns), jnp.bfloat16),
+            pltpu.SemaphoreType.DMA((4,)),
         ],
         cost_estimate=pl.CostEstimate(flops=flops, bytes_accessed=flops // 512, transcendentals=0),
         name="products",
@@ -191,17 +212,10 @@
     n_piece = len(widths)
     last = n_col - 1
 
-    bounds = lax.dynamic_slice_in_dim(offsets, own_row * per_dev, per_dev + 1)
-    lengths = bounds[1:] - bounds[:-1]
-    core_arg = core.astype(jnp.int32).reshape(1)
-
     swap = [(r, r ^ 1) for r in range(n_row)]
-    pieces = pack_coeffs(coeffs, lengths, core_arg, per_dev, atom_w, group, (half,))
-    paired = lax.ppermute(pieces[1], "row", swap)
-    units = []
-    for which in range(n_piece):
-        cut = slice(sum(widths[:which]), sum(widths[: which + 1]))
-        units.append(jnp.concatenate([pieces[0][:, cut], paired[:, cut]], axis=1))
+    other = lax.dynamic_slice_in_dim(coeffs, (1 - core) * half, half, axis=1)
+    paired = lax.ppermute(other, "row", swap)
+    units = pack_coeffs(coeffs, paired, offsets, own_row, per_dev, atom_w, group, widths)
 
     right = [(c, c + 1) for c in range(n_col - 1)]
     left = [(c + 1, c) for c in range(n_col - 1)]
@@ -209,6 +223,8 @@
     from_right = [lax.ppermute(unit, "col", left) for unit in units]
 
     table, where_of = block_tables(atom_of_slot, own_row, n_row, per_dev, slots)
+    bounds = lax.dynamic_slice_in_dim(offsets, own_row * per_dev, per_dev + 1)
+    lengths = bounds[1:] - bounds[:-1]
     alive = lax.dynamic_slice(mask, (own_row * per_dev, own_col), (per_dev, 1))[:, 0]
     outgoing = sort_blocks(integrals, table, n_chip, slots)
     arrived = [outgoing[0]] + [
@@ -242,7 +258,7 @@
         for d in range(1, n_chip):
             perm = [(r, r ^ (2 * d)) for r in range(n_row)]
             total = total + lax.ppermute(parts[d], "row", perm).astype(jnp.float32)
-        totals.append(total)
+        totals.append(lax.optimization_barrier(total.astype(jnp.bfloat16)))
 
     quarter = half // n_chip
     candidates = []
@@ -276,7 +292,7 @@
             jnp.where(on_left, given[q ^ last], given[q])
             for q in range(begin // quarter, (begin + width) // quarter)
         ]
-        rows.append(jnp.where(is_helped, jnp.concatenate(gifts), total.astype(jnp.bfloat16)))
+        rows.append(jnp.where(is_helped, jnp.concatenate(gifts), total))
         begin += width
     return jnp.concatenate(rows, axis=0)
 

time: 271 us -> 271 us (level)
  the two profiles are of different devices: /device:TPU:24 before, /device:TPU:6 now
where the time goes in v3:
time: 271 us; the launch traced here: 270 us
  waiting for transfers between devices  156 us (58%)
  starting transfers between devices  53 us (20%)
  Pallas kernels  43.8 us (16%)
  local copies, waits for them, and re-layouts  8.55 us (3%)
  other arithmetic  8.36 us (3%)
    ppermute x3, waiting for transfers between devices, line_body(): from_left = [lax.ppermute(unit, 'col', right) for unit in units]  41.1 us
    ppermute x12, waiting for transfers between devices, line_body(): total = total + lax.ppermute(parts[d], 'row', perm).astype(jnp.float32)  31.5 us
    pallas_call x4, Pallas kernels, products(): pl.pallas_call(functools.partial(products_kernel, candidates), in_specs=[...  30.2 us
    ppermute x3, waiting for transfers between devices, line_body(): far_right = [lax.ppermute(unit, 'col', left[:-1]) for unit in from_right]  26.5 us
    ppermute x3, waiting for transfers between devices, line_body(): lax.ppermute(outgoing[d], 'row', [(r, r ^ 2 * d) for r in range(n_row)])  26.5 us
    ppermute x3, waiting for transfers between devices, line_body(): from_right = [lax.ppermute(unit, 'col', left) for unit in units]  23.3 us
    ppermute x12, starting transfers between devices, line_body(): total = total + lax.ppermute(parts[d], 'row', perm).astype(jnp.float32)  14.7 us
    ppermute x3, starting transfers between devices, line_body(): from_left = [lax.ppermute(unit, 'col', right) for unit in units]  12.6 us
  transfers between devices with their start and end apart: 36, of which 11 were waited for; matrix products, arithmetic and copies ran while one was open for 3% of the time, Pallas kernels for 15%

profile of v3, /device:TPU:6, one launch (start us, length us, event | category | flops | bytes accessed | tf_op | source)
XLA Modules:
  0.0 270.1 jit_solution(12894916256943728409)
XLA Ops:
  2.6 3.4 %sort_blocks.1 = (bf16[10,32,1024]{2,1,0:T(8,128)(2,1)}, bf16[10,32,1024]{2,1,0:T(8,128)(2,1)}, bf16[10,32,1024]{2,1,0:T(8,128)(2,1)}, bf16[10,32,1024]{2,1,0:T(8,128)(2,1)}) custom-call(s32[40]{0:T(128)} %select_reduce_fusion.1.table, bf16[40,32,1024]{2,1,0:T(8,128)(2,1)} %blocks.1), custom_call_target="tpu_custom_call" | custom-call | tf_op jit(solution)/shard_map/sort_blocks/pallas_call | solution.py:77
  6.6 3.0 %collective-permute-start.2 = (bf16[10,32,1024]{2,1,0:T(8,128)(2,1)}, bf16[10,32,1024]{2,1,0:T(8,128)(2,1)S(1)}, u32[]{:S(2)}, u32[]{:S(2)}) collective-permute-start(bf16[10,32,1024]{2,1,0:T(8,128)(2,1)} %get-tuple-element.31), channel_id=1, source_target_pairs={{0,24},{4,28},{8,16},{12,20},{16,8},{20,12},{24,0},{28,4},{1,25},{... | collective-permute-start | bytes 1966088 | tf_op jit(solution)/shard_map/ppermute | solution.py:231
  10.5 13.3 %collective-permute-done.refs_1_ = bf16[10,32,1024]{2,1,0:T(8,128)(2,1)S(1)} collective-permute-done((bf16[10,32,1024]{2,1,0:T(8,128)(2,1)}, bf16[10,32,1024]{2,1,0:T(8,128)(2,1)S(1)}, u32[]{:S(2)}, u32[]{:S(2)}) %collective-permute-start) | collective-permute-done | bytes 655392 | tf_op jit(solution)/shard_map/ppermute | solution.py:231
  23.9 13.1 %collective-permute-done.1.refs_2_ = bf16[10,32,1024]{2,1,0:T(8,128)(2,1)S(1)} collective-permute-done((bf16[10,32,1024]{2,1,0:T(8,128)(2,1)}, bf16[10,32,1024]{2,1,0:T(8,128)(2,1)S(1)}, u32[]{:S(2)}, u32[]{:S(2)}) %collective-permute-start.1) | collective-permute-done | bytes 655392 | tf_op jit(solution)/shard_map/ppermute | solution.py:231
  44.6 4.3 %pack_kept.1.kept = bf16[960,1024]{1,0:T(8,128)(2,1)} custom-call(s32[40]{0:T(128)} %select_reduce_fusion.where_of, s32[40]{0:T(128)} %slice_subtract_fusion.lengths, s32[40]{0:T(128)} %dynamic-slice_bitcast_fusion.alive, bf16[10,32,1024]{2,1,0:T(8,128)(2,1)} %get-tuple-element.28.refs_0_, bf16[10,32,1024]{2,1,0:T(8,128)(2,1)} %copy-done.3, ...), custom_call_target="tpu_custom_call" | custom-call | tf_op jit(solution)/shard_map/pack_kept/pallas_call | solution.py:107
  48.9 4.7 %collective-permute-start.4 = (bf16[960,1024]{1,0:T(8,128)(2,1)}, bf16[960,1024]{1,0:T(8,128)(2,1)}, u32[]{:S(2)}, u32[]{:S(2)}) collective-permute-start(bf16[960,1024]{1,0:T(8,128)(2,1)} %pack_kept.1.kept), channel_id=1, source_target_pairs={{0,1},{3,2},{4,5},{7,6},{8,9},{11,10},{12,13},{15,14},{16,17},{19,... | collective-permute-start | bytes 5898248 | tf_op jit(solution)/shard_map/ppermute | solution.py:242
  54.7 5.8 %pack_coeffs.1 = (bf16[960,512]{1,0:T(8,128)(2,1)}, bf16[960,256]{1,0:T(8,128)(2,1)}, bf16[960,256]{1,0:T(8,128)(2,1)}) custom-call(s32[1]{0:T(128)} %bitcast.2.place, s32[321]{0:T(512)} %offsets.1, bf16[1280,1024]{1,0:T(8,128)(2,1)} %mine.1, bf16[1280,512]{1,0:T(8,128)(2,1)} %copy-done.6), custom_call_target="tpu_custom_call" | custom-call | tf_op jit(solution)/shard_map/pack_coeffs/pallas_call | solution.py:48
  63.3 5.3 %collective-permute-start.11 = (bf16[960,256]{1,0:T(8,128)(2,1)}, bf16[960,256]{1,0:T(8,128)(2,1)}, u32[]{:S(2)}, u32[]{:S(2)}) collective-permute-start(bf16[960,256]{1,0:T(8,128)(2,1)} %get-tuple-element.34.refs_0_), channel_id=1, source_target_pairs={{0,1},{1,2},{2,3},{4,5},{5,6},{6,7},{8,9},{9,10},{10,11},{12,13},{... | collective-permute-start | bytes 1474568 | tf_op jit(solution)/shard_map/ppermute | solution.py:222
  68.6 37.8 %collective-permute-done.9.refs_1_ = bf16[960,256]{1,0:T(8,128)(2,1)S(1)} collective-permute-done((bf16[960,256]{1,0:T(8,128)(2,1)}, bf16[960,256]{1,0:T(8,128)(2,1)S(1)}, u32[]{:S(2)}, u32[]{:S(2)}) %collective-permute-start.9) | collective-permute-done | bytes 491552 | tf_op jit(solution)/shard_map/ppermute | solution.py:222
  107.8 5.9 %collective-permute-start.7 = (bf16[960,512]{1,0:T(8,128)(2,1)}, bf16[960,512]{1,0:T(8,128)(2,1)}, u32[]{:S(2)}, u32[]{:S(2)}) collective-permute-start(bf16[960,512]{1,0:T(8,128)(2,1)} %get-tuple-element.32.refs_0_), channel_id=1, source_target_pairs={{0,1},{1,2},{2,3},{4,5},{5,6},{6,7},{8,9},{9,10},{10,11},{12,13},{... | collective-permute-start | bytes 2949128 | tf_op jit(solution)/shard_map/ppermute | solution.py:222
  113.7 3.3 %collective-permute-done.11.refs_1_ = bf16[960,256]{1,0:T(8,128)(2,1)} collective-permute-done((bf16[960,256]{1,0:T(8,128)(2,1)}, bf16[960,256]{1,0:T(8,128)(2,1)}, u32[]{:S(2)}, u32[]{:S(2)}) %collective-permute-start.11) | collective-permute-done | bytes 491552 | tf_op jit(solution)/shard_map/ppermute | solution.py:222
  118.4 23.3 %collective-permute-done.17.refs_2_ = bf16[960,256]{1,0:T(8,128)(2,1)} collective-permute-done((bf16[960,256]{1,0:T(8,128)(2,1)}, bf16[960,256]{1,0:T(8,128)(2,1)}, u32[]{:S(2)}, u32[]{:S(2)}) %collective-permute-start.17) | collective-permute-done | bytes 491552 | tf_op jit(solution)/shard_map/ppermute | solution.py:223
  146.7 12.2 %collective-permute-done.16.refs_4_ = bf16[960,256]{1,0:T(8,128)(2,1)S(1)} collective-permute-done((bf16[960,256]{1,0:T(8,128)(2,1)S(1)}, bf16[960,256]{1,0:T(8,128)(2,1)S(1)}, u32[]{:S(2)}, u32[]{:S(2)}) %collective-permute-start.16) | collective-permute-done | bytes 491552 | tf_op jit(solution)/shard_map/ppermute | solution.py:240
  164.3 6.8 %products.6 = (bf16[128,1024]{1,0:T(8,128)(2,1)}, bf16[128,1024]{1,0:T(8,128)(2,1)}, bf16[128,1024]{1,0:T(8,128)(2,1)}, bf16[128,1024]{1,0:T(8,128)(2,1)}) custom-call(s32[4]{0:T(128)} %compare_select_fusion.3.choice, bf16[960,1024]{1,0:T(8,128)(2,1)} %pack_kept.1.kept, bf16[960,1024]{1,0:T(8,128)(2,1)} %copy-done.15, ...), custom_call_target="tpu_custom_call" | custom-call | flops 2013265920 | bytes 3932160 | tf_op jit(solution)/shard_map/products/pallas_call | solution.py:186
  172.7 14.3 %collective-permute-done.18.refs_5_.refs_4_ = bf16[960,256]{1,0:T(8,128)(2,1)S(1)} collective-permute-done((bf16[960,256]{1,0:T(8,128)(2,1)}, bf16[960,256]{1,0:T(8,128)(2,1)S(1)}, u32[]{:S(2)}, u32[]{:S(2)}) %collective-permute-start.18) | collective-permute-done | bytes 491552 | tf_op jit(solution)/shard_map/ppermute | solution.py:240
  187.8 6.8 %products.7 = (bf16[128,1024]{1,0:T(8,128)(2,1)}, bf16[128,1024]{1,0:T(8,128)(2,1)}, bf16[128,1024]{1,0:T(8,128)(2,1)}, bf16[128,1024]{1,0:T(8,128)(2,1)}) custom-call(s32[4]{0:T(128)} %compare_select_fusion.3.choice, bf16[960,1024]{1,0:T(8,128)(2,1)} %pack_kept.1.kept, bf16[960,1024]{1,0:T(8,128)(2,1)} %copy-done.15, ...), custom_call_target="tpu_custom_call" | custom-call | flops 2013265920 | bytes 3932160 | tf_op jit(solution)/shard_map/products/pallas_call | solution.py:186
  194.6 2.2 collective-permute-start.32
  198.2 6.9 %products.4 = (bf16[128,1024]{1,0:T(8,128)(2,1)}, bf16[128,1024]{1,0:T(8,128)(2,1)}, bf16[128,1024]{1,0:T(8,128)(2,1)}, bf16[128,1024]{1,0:T(8,128)(2,1)}) custom-call(s32[4]{0:T(128)} %multiply_add_fusion.choice, bf16[960,1024]{1,0:T(8,128)(2,1)} %collective-permute-done.4.kept, bf16[960,1024]{1,0:T(8,128)(2,1)} %collective-permute-done.5.kept_pair, ...), custom_call_target="tpu_custom_call" | custom-call | flops 2013265920 | bytes 3932160 | tf_op jit(solution)/shard_map/products/pallas_call | solution.py:186
  205.1 2.2 collective-permute-start.35
  207.9 9.7 %products.5 = (bf16[256,1024]{1,0:T(8,128)(2,1)}, bf16[256,1024]{1,0:T(8,128)(2,1)}, bf16[256,1024]{1,0:T(8,128)(2,1)}, bf16[256,1024]{1,0:T(8,128)(2,1)}) custom-call(s32[4]{0:T(128)} %compare_select_fusion.3.choice, bf16[960,1024]{1,0:T(8,128)(2,1)} %pack_kept.1.kept, bf16[960,1024]{1,0:T(8,128)(2,1)} %copy-done.15, ...), custom_call_target="tpu_custom_call" | custom-call | flops 4026531840 | bytes 7864320 | tf_op jit(solution)/shard_map/products/pallas_call | solution.py:186
  222.0 2.1 collective-permute-start.21
  224.5 31.4 %collective-permute-done.20 = bf16[128,1024]{1,0:T(8,128)(2,1)S(1)} collective-permute-done((bf16[128,1024]{1,0:T(8,128)(2,1)}, bf16[128,1024]{1,0:T(8,128)(2,1)S(1)}, u32[]{:S(2)}, u32[]{:S(2)}) %collective-permute-start.20) | collective-permute-done | bytes 262176 | tf_op jit(solution)/shard_map/ppermute | solution.py:278
  261.8 3.5 %collective-permute-done.24 = bf16[128,1024]{1,0:T(8,128)(2,1)S(1)} collective-permute-done((bf16[128,1024]{1,0:T(8,128)(2,1)S(1)}, bf16[128,1024]{1,0:T(8,128)(2,1)S(1)}, u32[]{:S(2)}, u32[]{:S(2)}) %collective-permute-start.24) | collective-permute-done | bytes 262176 | tf_op jit(solution)/shard_map/ppermute | solution.py:287
  266.7 2.2 collective-permute-done.22
  (125 shorter events, 45.8 us)
Async XLA Ops:
  6.6 30.4 %collective-permute-start.1 = (bf16[10,32,1024]{2,1,0:T(8,128)(2,1)}, bf16[10,32,1024]{2,1,0:T(8,128)(2,1)S(1)}, u32[]{:S(2)}, u32[]{:S(2)}) collective-permute-start(bf16[10,32,1024]{2,1,0:T(8,128)(2,1)} %get-tuple-element.30), channel_id=1, source_target_pairs={{0,16},{4,20},{8,24},{12,28},{16,0},{20,4},{24,8},{28,12},{1,17},{... | collective-permute-start | bytes 1966088 | tf_op jit(solution)/shard_map/ppermute | solution.py:231
  6.6 31.3 %collective-permute-start.2 = (bf16[10,32,1024]{2,1,0:T(8,128)(2,1)}, bf16[10,32,1024]{2,1,0:T(8,128)(2,1)S(1)}, u32[]{:S(2)}, u32[]{:S(2)}) collective-permute-start(bf16[10,32,1024]{2,1,0:T(8,128)(2,1)} %get-tuple-element.31), channel_id=1, source_target_pairs={{0,24},{4,28},{8,16},{12,20},{16,8},{20,12},{24,0},{28,4},{1,25},{... | collective-permute-start | bytes 1966088 | tf_op jit(solution)/shard_map/ppermute | solution.py:231
  48.9 69.3 %collective-permute-start.4 = (bf16[960,1024]{1,0:T(8,128)(2,1)}, bf16[960,1024]{1,0:T(8,128)(2,1)}, u32[]{:S(2)}, u32[]{:S(2)}) collective-permute-start(bf16[960,1024]{1,0:T(8,128)(2,1)} %pack_kept.1.kept), channel_id=1, source_target_pairs={{0,1},{3,2},{4,5},{7,6},{8,9},{11,10},{12,13},{15,14},{16,17},{19,... | collective-permute-start | bytes 5898248 | tf_op jit(solution)/shard_map/ppermute | solution.py:242
  60.6 45.9 %collective-permute-start.9 = (bf16[960,256]{1,0:T(8,128)(2,1)}, bf16[960,256]{1,0:T(8,128)(2,1)S(1)}, u32[]{:S(2)}, u32[]{:S(2)}) collective-permute-start(bf16[960,256]{1,0:T(8,128)(2,1)} %get-tuple-element.33.refs_0_), channel_id=1, source_target_pairs={{0,1},{1,2},{2,3},{4,5},{5,6},{6,7},{8,9},{9,10},{10,11},{12,13},{... | collective-permute-start | bytes 1474568 | tf_op jit(solution)/shard_map/ppermute | solution.py:222
  61.9 98.4 %collective-permute-start.26 = (bf16[960,1024]{1,0:T(8,128)(2,1)S(1)}, bf16[960,1024]{1,0:T(8,128)(2,1)S(1)}, u32[]{:S(2)}, u32[]{:S(2)}) collective-permute-start(bf16[960,1024]{1,0:T(8,128)(2,1)S(1)} %copy-done.2), channel_id=1, source_target_pairs={{0,4},{4,0},{8,12},{12,8},{16,20},{20,16},{24,28},{28,24},{1,5},{5... | collective-permute-start | bytes 5898248 | tf_op jit(solution)/shard_map/ppermute | solution.py:237
  62.0 45.7 %collective-permute-start.15 = (bf16[960,256]{1,0:T(8,128)(2,1)}, bf16[960,256]{1,0:T(8,128)(2,1)S(1)}, u32[]{:S(2)}, u32[]{:S(2)}) collective-permute-start(bf16[960,256]{1,0:T(8,128)(2,1)} %get-tuple-element.33.refs_0_), channel_id=1, source_target_pairs={{1,0},{2,1},{3,2},{5,4},{6,5},{7,6},{9,8},{10,9},{11,10},{13,12},{... | collective-permute-start | bytes 1474568 | tf_op jit(solution)/shard_map/ppermute | solution.py:223
  63.3 53.7 %collective-permute-start.11 = (bf16[960,256]{1,0:T(8,128)(2,1)}, bf16[960,256]{1,0:T(8,128)(2,1)}, u32[]{:S(2)}, u32[]{:S(2)}) collective-permute-start(bf16[960,256]{1,0:T(8,128)(2,1)} %get-tuple-element.34.refs_0_), channel_id=1, source_target_pairs={{0,1},{1,2},{2,3},{4,5},{5,6},{6,7},{8,9},{9,10},{10,11},{12,13},{... | collective-permute-start | bytes 1474568 | tf_op jit(solution)/shard_map/ppermute | solution.py:222
  106.5 35.9 %collective-permute-start.13 = (bf16[960,512]{1,0:T(8,128)(2,1)}, bf16[960,512]{1,0:T(8,128)(2,1)}, u32[]{:S(2)}, u32[]{:S(2)}) collective-permute-start(bf16[960,512]{1,0:T(8,128)(2,1)} %get-tuple-element.32.refs_0_), channel_id=1, source_target_pairs={{1,0},{2,1},{3,2},{5,4},{6,5},{7,6},{9,8},{10,9},{11,10},{13,12},{... | collective-permute-start | bytes 2949128 | tf_op jit(solution)/shard_map/ppermute | solution.py:223
  107.8 35.9 %collective-permute-start.7 = (bf16[960,512]{1,0:T(8,128)(2,1)}, bf16[960,512]{1,0:T(8,128)(2,1)}, u32[]{:S(2)}, u32[]{:S(2)}) collective-permute-start(bf16[960,512]{1,0:T(8,128)(2,1)} %get-tuple-element.32.refs_0_), channel_id=1, source_target_pairs={{0,1},{1,2},{2,3},{4,5},{5,6},{6,7},{8,9},{9,10},{10,11},{12,13},{... | collective-permute-start | bytes 2949128 | tf_op jit(solution)/shard_map/ppermute | solution.py:222
  117.0 24.7 %collective-permute-start.17 = (bf16[960,256]{1,0:T(8,128)(2,1)}, bf16[960,256]{1,0:T(8,128)(2,1)}, u32[]{:S(2)}, u32[]{:S(2)}) collective-permute-start(bf16[960,256]{1,0:T(8,128)(2,1)} %get-tuple-element.34.refs_0_), channel_id=1, source_target_pairs={{1,0},{2,1},{3,2},{5,4},{6,5},{7,6},{9,8},{10,9},{11,10},{13,12},{... | collective-permute-start | bytes 1474568 | tf_op jit(solution)/shard_map/ppermute | solution.py:223
  118.3 79.1 %collective-permute-start.5 = (bf16[960,1024]{1,0:T(8,128)(2,1)}, bf16[960,1024]{1,0:T(8,128)(2,1)}, u32[]{:S(2)}, u32[]{:S(2)}) collective-permute-start(bf16[960,1024]{1,0:T(8,128)(2,1)} %collective-permute-done.4.kept), channel_id=1, source_target_pairs={{0,4},{4,0},{8,12},{12,8},{16,20},{20,16},{24,28},{28,24},{1,5},{5... | collective-permute-start | bytes 5898248 | tf_op jit(solution)/shard_map/ppermute | solution.py:243
  143.7 50.9 %collective-permute-start.14 = (bf16[960,512]{1,0:T(8,128)(2,1)}, bf16[960,512]{1,0:T(8,128)(2,1)S(1)}, u32[]{:S(2)}, u32[]{:S(2)}) collective-permute-start(bf16[960,512]{1,0:T(8,128)(2,1)} %collective-permute-done.13.refs_2_), channel_id=1, source_target_pairs={{1,0},{2,1},{5,4},{6,5},{9,8},{10,9},{13,12},{14,13},{17,16},{18,1... | collective-permute-start | bytes 2949128 | tf_op jit(solution)/shard_map/ppermute | solution.py:240
  145.0 51.8 %collective-permute-start.8 = (bf16[960,512]{1,0:T(8,128)(2,1)}, bf16[960,512]{1,0:T(8,128)(2,1)}, u32[]{:S(2)}, u32[]{:S(2)}) collective-permute-start(bf16[960,512]{1,0:T(8,128)(2,1)} %collective-permute-done.7.refs_1_), channel_id=1, source_target_pairs={{1,2},{2,3},{5,6},{6,7},{9,10},{10,11},{13,14},{14,15},{17,18},{18... | collective-permute-start | bytes 2949128 | tf_op jit(solution)/shard_map/ppermute | solution.py:239
  161.7 25.3 %collective-permute-start.18 = (bf16[960,256]{1,0:T(8,128)(2,1)}, bf16[960,256]{1,0:T(8,128)(2,1)S(1)}, u32[]{:S(2)}, u32[]{:S(2)}) collective-permute-start(bf16[960,256]{1,0:T(8,128)(2,1)} %collective-permute-done.17.refs_2_), channel_id=1, source_target_pairs={{1,0},{2,1},{5,4},{6,5},{9,8},{10,9},{13,12},{14,13},{17,16},{18,1... | collective-permute-start | bytes 1474568 | tf_op jit(solution)/shard_map/ppermute | solution.py:240
  171.2 33.9 %collective-permute-start.30 = (bf16[128,1024]{1,0:T(8,128)(2,1)}, bf16[128,1024]{1,0:T(8,128)(2,1)S(1)}, u32[]{:S(2)}, u32[]{:S(2)}) collective-permute-start(bf16[128,1024]{1,0:T(8,128)(2,1)} %get-tuple-element.44), channel_id=1, source_target_pairs={{0,8},{4,12},{8,0},{12,4},{16,24},{20,28},{24,16},{28,20},{1,9},{5... | collective-permute-start | bytes 786440 | tf_op jit(solution)/shard_map/ppermute | solution.py:260
  187.0 20.3 %collective-permute-start.31 = (bf16[128,1024]{1,0:T(8,128)(2,1)}, bf16[128,1024]{1,0:T(8,128)(2,1)S(1)}, u32[]{:S(2)}, u32[]{:S(2)}) collective-permute-start(bf16[128,1024]{1,0:T(8,128)(2,1)} %get-tuple-element.45), channel_id=1, source_target_pairs={{0,16},{4,20},{8,24},{12,28},{16,0},{20,4},{24,8},{28,12},{1,17},{... | collective-permute-start | bytes 786440 | tf_op jit(solution)/shard_map/ppermute | solution.py:260
  194.6 23.0 %collective-permute-start.32 = (bf16[128,1024]{1,0:T(8,128)(2,1)}, bf16[128,1024]{1,0:T(8,128)(2,1)S(1)}, u32[]{:S(2)}, u32[]{:S(2)}) collective-permute-start(bf16[128,1024]{1,0:T(8,128)(2,1)} %get-tuple-element.46), channel_id=1, source_target_pairs={{0,24},{4,28},{8,16},{12,20},{16,8},{20,12},{24,0},{28,4},{1,25},{... | collective-permute-start | bytes 786440 | tf_op jit(solution)/shard_map/ppermute | solution.py:260
  196.9 22.3 %collective-permute-start.33 = (bf16[128,1024]{1,0:T(8,128)(2,1)}, bf16[128,1024]{1,0:T(8,128)(2,1)S(1)}, u32[]{:S(2)}, u32[]{:S(2)}) collective-permute-start(bf16[128,1024]{1,0:T(8,128)(2,1)} %get-tuple-element.48), channel_id=1, source_target_pairs={{0,8},{4,12},{8,0},{12,4},{16,24},{20,28},{24,16},{28,20},{1,9},{5... | collective-permute-start | bytes 786440 | tf_op jit(solution)/shard_map/ppermute | solution.py:260
  197.4 22.5 %collective-permute-start.34 = (bf16[128,1024]{1,0:T(8,128)(2,1)}, bf16[128,1024]{1,0:T(8,128)(2,1)S(1)}, u32[]{:S(2)}, u32[]{:S(2)}) collective-permute-start(bf16[128,1024]{1,0:T(8,128)(2,1)} %get-tuple-element.49), channel_id=1, source_target_pairs={{0,16},{4,20},{8,24},{12,28},{16,0},{20,4},{24,8},{28,12},{1,17},{... | collective-permute-start | bytes 786440 | tf_op jit(solution)/shard_map/ppermute | solution.py:260
  217.7 41.1 %collective-permute-start.27 = (bf16[256,1024]{1,0:T(8,128)(2,1)}, bf16[256,1024]{1,0:T(8,128)(2,1)S(1)}, u32[]{:S(2)}, u32[]{:S(2)}) collective-permute-start(bf16[256,1024]{1,0:T(8,128)(2,1)} %get-tuple-element.40), channel_id=1, source_target_pairs={{0,8},{4,12},{8,0},{12,4},{16,24},{20,28},{24,16},{28,20},{1,9},{5... | collective-permute-start | bytes 1572872 | tf_op jit(solution)/shard_map/ppermute | solution.py:260
  219.2 40.9 %collective-permute-start.28 = (bf16[256,1024]{1,0:T(8,128)(2,1)}, bf16[256,1024]{1,0:T(8,128)(2,1)S(1)}, u32[]{:S(2)}, u32[]{:S(2)}) collective-permute-start(bf16[256,1024]{1,0:T(8,128)(2,1)} %get-tuple-element.41), channel_id=1, source_target_pairs={{0,16},{4,20},{8,24},{12,28},{16,0},{20,4},{24,8},{28,12},{1,17},{... | collective-permute-start | bytes 1572872 | tf_op jit(solution)/shard_map/ppermute | solution.py:260
  220.0 41.4 %collective-permute-start.29 = (bf16[256,1024]{1,0:T(8,128)(2,1)}, bf16[256,1024]{1,0:T(8,128)(2,1)S(1)}, u32[]{:S(2)}, u32[]{:S(2)}) collective-permute-start(bf16[256,1024]{1,0:T(8,128)(2,1)} %get-tuple-element.42), channel_id=1, source_target_pairs={{0,24},{4,28},{8,16},{12,20},{16,8},{20,12},{24,0},{28,4},{1,25},{... | collective-permute-start | bytes 1572872 | tf_op jit(solution)/shard_map/ppermute | solution.py:260
  221.2 34.7 %collective-permute-start.20 = (bf16[128,1024]{1,0:T(8,128)(2,1)}, bf16[128,1024]{1,0:T(8,128)(2,1)S(1)}, u32[]{:S(2)}, u32[]{:S(2)}) collective-permute-start(bf16[128,1024]{1,0:T(8,128)(2,1)} %get-tuple-element.37), channel_id=1, source_target_pairs={{0,16},{4,20},{8,24},{12,28},{16,0},{20,4},{24,8},{28,12},{1,17},{... | collective-permute-start | bytes 786440 | tf_op jit(solution)/shard_map/ppermute | solution.py:278
  222.0 33.9 %collective-permute-start.21 = (bf16[128,1024]{1,0:T(8,128)(2,1)S(1)}, bf16[128,1024]{1,0:T(8,128)(2,1)S(1)}, u32[]{:S(2)}, u32[]{:S(2)}) collective-permute-start(bf16[128,1024]{1,0:T(8,128)(2,1)S(1)} %copy-done.18), channel_id=1, source_target_pairs={{0,24},{4,28},{8,16},{12,20},{16,8},{20,12},{24,0},{28,4},{1,25},{... | collective-permute-start | bytes 786440 | tf_op jit(solution)/shard_map/ppermute | solution.py:278
  (31 other events, 478.3 us)

commit v4 on v3

--- a/solution.py
+++ b/solution.py
@@ -11,55 +11,64 @@
 
 
 def selector(first, alive, atom_w, group):
-    pair_w = 3 * atom_w // 2
-    rows, cols = group // 2 * pair_w, group * atom_w
-    row = lax.broadcasted_iota(jnp.int32, (rows, cols), 0)
-    col = lax.broadcasted_iota(jnp.int32, (rows, cols), 1)
-    wanted = jnp.full((rows, cols), -1, jnp.int32)
+    pair_w, cols = 3 * atom_w // 2, group * atom_w
+    row = lax.broadcasted_iota(jnp.int32, (pair_w, cols), 0)
+    col = lax.broadcasted_iota(jnp.int32, (pair_w, cols), 1)
+    bands = []
     for pair in range(group // 2):
-        inside = row - pair * pair_w
-        in_first = inside < first[pair]
-        source = jnp.where(in_first, inside, inside + atom_w - first[pair]) + 2 * pair * atom_w
+        in_first = row < first[pair]
+        source = row + jnp.where(in_first, 0, atom_w - first[pair])
+        hit = source == col - 2 * pair * atom_w
         if alive is not None:
-            live = jnp.where(in_first, alive[2 * pair], alive[2 * pair + 1]) > 0
-            source = jnp.where(live, source, -1)
-        wanted = jnp.where((inside >= 0) & (inside < pair_w), source, wanted)
-    return (wanted == col).astype(jnp.bfloat16)
-
-
-def pack_coeffs_kernel(atom_w, group, per_dev, widths, place, offsets, mine, paired, *pieces):
-    step = pl.program_id(0)
-    for side, block in enumerate((mine, paired)):
-        base = (place[0] if side == 0 else place[0] ^ 1) * per_dev + step * group
-        marks = [offsets[base + atom] for atom in range(group)]
-        first = [marks[2 * pair + 1] - marks[2 * pair] for pair in range(group // 2)]
-        chooser = selector(first, None, atom_w, group)
-        begin = 0
-        for piece, width in zip(pieces, widths):
-            piece[:, side * width : (side + 1) * width] = jnp.dot(
-                chooser, block[:, begin : begin + width], preferred_element_type=jnp.float32
-            ).astype(jnp.bfloat16)
-            begin += width
+            live = jnp.where(in_first, alive[2 * pair], alive[2 * pair + 1])
+            hit = hit & (live > 0)
+        bands.append(jnp.where(hit, 1.0, 0.0).astype(jnp.bfloat16))
+    return jnp.concatenate(bands, axis=0)
+
+
+def pack_coeffs_kernel(atom_w, group, per_dev, widths, here, offsets, coeffs, paired, *refs):
+    pieces, held, sems = refs[:-2], refs[-2], refs[-1]
+    rows_in, rows_out = group * atom_w, group // 2 * (3 * atom_w // 2)
+    half = held.shape[2]
+    column = pl.multiple_of(here[0] % 2 * half, half)
+    loads = []
+    for step in range(per_dev // group):
+        rows = pl.ds(step * rows_in, rows_in)
+        for side, source in enumerate((coeffs.at[rows, pl.ds(column, half)], paired.at[rows])):
+            load = pltpu.make_async_copy(source, held.at[side, rows], sems.at[2 * step + side])
+            load.start()
+            loads.append(load)
+    for step in range(per_dev // group):
+        for side in range(2):
+            base = (here[0] ^ side) * per_dev + step * group
+            marks = [offsets[base + atom] for atom in range(group)]
+            first = [marks[2 * pair + 1] - marks[2 * pair] for pair in range(group // 2)]
+            chooser = selector(first, None, atom_w, group)
+            loads[2 * step + side].wait()
+            block = held[side, step * rows_in : (step + 1) * rows_in]
+            packed = jnp.dot(chooser, block, preferred_element_type=jnp.float32)
+            packed = packed.astype(jnp.bfloat16)
+            begin = 0
+            for piece, width in zip(pieces, widths):
+                piece[
+                    step * rows_out : (step + 1) * rows_out, side * width : (side + 1) * width
+                ] = packed[:, begin : begin + width]
+                begin += width
 
 
 def pack_coeffs(coeffs, paired, offsets, own_row, per_dev, atom_w, group, widths):
-    rows_in, rows_out = group * atom_w, group // 2 * (3 * atom_w // 2)
-    steps, half = per_dev // group, paired.shape[1]
+    steps, rows_out = per_dev // group, group // 2 * (3 * atom_w // 2)
+    smem, vmem = pl.BlockSpec(memory_space=pltpu.SMEM), pl.BlockSpec(memory_space=pltpu.VMEM)
     return pl.pallas_call(
         functools.partial(pack_coeffs_kernel, atom_w, group, per_dev, widths),
-        grid_spec=pltpu.PrefetchScalarGridSpec(
-            num_scalar_prefetch=2,
-            grid=(steps,),
-            in_specs=[
-                pl.BlockSpec((rows_in, half), lambda i, place, offsets: (i, place[0] % 2)),
-                pl.BlockSpec((rows_in, half), lambda i, place, offsets: (i, 0)),
-            ],
-            out_specs=[
-                pl.BlockSpec((rows_out, 2 * w), lambda i, place, offsets: (i, 0)) for w in widths
-            ],
-        ),
+        in_specs=[smem, smem] + [pl.BlockSpec(memory_space=pl.ANY)] * 2,
+        out_specs=[vmem] * len(widths),
         out_shape=[
             jax.ShapeDtypeStruct((steps * rows_out, 2 * w), jnp.bfloat16) for w in widths
+        ],
+        scratch_shapes=[
+            pltpu.VMEM((2,) + paired.shape, jnp.bfloat16),
+            pltpu.SemaphoreType.DMA((2 * steps,)),
         ],
         name="pack_coeffs",
     )(own_row.astype(jnp.int32).reshape(1), offsets, coeffs, paired)

time: 271 us -> 271 us (level)
  no operation moved by 1% of the time
where the time goes in v4:
time: 271 us; the launch traced here: 270 us
  waiting for transfers between devices  156 us (58%)
  starting transfers between devices  53.1 us (20%)
  Pallas kernels  43.3 us (16%)
  local copies, waits for them, and re-layouts  8.54 us (3%)
  other arithmetic  8.36 us (3%)
    ppermute x3, waiting for transfers between devices, line_body(): from_left = [lax.ppermute(unit, 'col', right) for unit in units]  41.6 us
    ppermute x12, waiting for transfers between devices, line_body(): total = total + lax.ppermute(parts[d], 'row', perm).astype(jnp.float32)  31.5 us
    pallas_call x4, Pallas kernels, products(): pl.pallas_call(functools.partial(products_kernel, candidates), in_specs=[...  30.2 us
    ppermute x3, waiting for transfers between devices, line_body(): lax.ppermute(outgoing[d], 'row', [(r, r ^ 2 * d) for r in range(n_row)])  26.5 us
    ppermute x3, waiting for transfers between devices, line_body(): far_right = [lax.ppermute(unit, 'col', left[:-1]) for unit in from_right]  26.5 us
    ppermute x3, waiting for transfers between devices, line_body(): from_right = [lax.ppermute(unit, 'col', left) for unit in units]  23.3 us
    ppermute x12, starting transfers between devices, line_body(): total = total + lax.ppermute(parts[d], 'row', perm).astype(jnp.float32)  14.8 us
    ppermute x3, starting transfers between devices, line_body(): from_left = [lax.ppermute(unit, 'col', right) for unit in units]  12.6 us
  transfers between devices with their start and end apart: 36, of which 11 were waited for; matrix products, arithmetic and copies ran while one was open for 3% of the time, Pallas kernels for 15%

profile of v4, /device:TPU:6, one launch (start us, length us, event | category | flops | bytes accessed | tf_op | source)
XLA Modules:
  0.0 270.1 jit_solution(15037155821652602242)
XLA Ops:
  2.6 3.4 %sort_blocks.1 = (bf16[10,32,1024]{2,1,0:T(8,128)(2,1)}, bf16[10,32,1024]{2,1,0:T(8,128)(2,1)}, bf16[10,32,1024]{2,1,0:T(8,128)(2,1)}, bf16[10,32,1024]{2,1,0:T(8,128)(2,1)}) custom-call(s32[40]{0:T(128)} %select_reduce_fusion.1.table, bf16[40,32,1024]{2,1,0:T(8,128)(2,1)} %blocks.1), custom_call_target="tpu_custom_call" | custom-call | tf_op jit(solution)/shard_map/sort_blocks/pallas_call | solution.py:86
  6.6 3.0 %collective-permute-start.2 = (bf16[10,32,1024]{2,1,0:T(8,128)(2,1)}, bf16[10,32,1024]{2,1,0:T(8,128)(2,1)S(1)}, u32[]{:S(2)}, u32[]{:S(2)}) collective-permute-start(bf16[10,32,1024]{2,1,0:T(8,128)(2,1)} %get-tuple-element.31), channel_id=1, source_target_pairs={{0,24},{4,28},{8,16},{12,20},{16,8},{20,12},{24,0},{28,4},{1,25},{... | collective-permute-start | bytes 1966088 | tf_op jit(solution)/shard_map/ppermute | solution.py:240
  10.5 13.3 %collective-permute-done.refs_1_ = bf16[10,32,1024]{2,1,0:T(8,128)(2,1)S(1)} collective-permute-done((bf16[10,32,1024]{2,1,0:T(8,128)(2,1)}, bf16[10,32,1024]{2,1,0:T(8,128)(2,1)S(1)}, u32[]{:S(2)}, u32[]{:S(2)}) %collective-permute-start) | collective-permute-done | bytes 655392 | tf_op jit(solution)/shard_map/ppermute | solution.py:240
  23.9 13.1 %collective-permute-done.1.refs_2_ = bf16[10,32,1024]{2,1,0:T(8,128)(2,1)S(1)} collective-permute-done((bf16[10,32,1024]{2,1,0:T(8,128)(2,1)}, bf16[10,32,1024]{2,1,0:T(8,128)(2,1)S(1)}, u32[]{:S(2)}, u32[]{:S(2)}) %collective-permute-start.1) | collective-permute-done | bytes 655392 | tf_op jit(solution)/shard_map/ppermute | solution.py:240
  44.6 4.3 %pack_kept.1.kept = bf16[960,1024]{1,0:T(8,128)(2,1)} custom-call(s32[40]{0:T(128)} %select_reduce_fusion.where_of, s32[40]{0:T(128)} %slice_subtract_fusion.lengths, s32[40]{0:T(128)} %dynamic-slice_bitcast_fusion.alive, bf16[10,32,1024]{2,1,0:T(8,128)(2,1)} %get-tuple-element.28.refs_0_, bf16[10,32,1024]{2,1,0:T(8,128)(2,1)} %copy-done.3, ...), custom_call_target="tpu_custom_call" | custom-call | tf_op jit(solution)/shard_map/pack_kept/pallas_call | solution.py:116
  48.9 4.7 %collective-permute-start.4 = (bf16[960,1024]{1,0:T(8,128)(2,1)}, bf16[960,1024]{1,0:T(8,128)(2,1)}, u32[]{:S(2)}, u32[]{:S(2)}) collective-permute-start(bf16[960,1024]{1,0:T(8,128)(2,1)} %pack_kept.1.kept), channel_id=1, source_target_pairs={{0,1},{3,2},{4,5},{7,6},{8,9},{11,10},{12,13},{15,14},{16,17},{19,... | collective-permute-start | bytes 5898248 | tf_op jit(solution)/shard_map/ppermute | solution.py:251
  54.7 5.4 %pack_coeffs.1 = (bf16[960,512]{1,0:T(8,128)(2,1)}, bf16[960,256]{1,0:T(8,128)(2,1)}, bf16[960,256]{1,0:T(8,128)(2,1)}) custom-call(s32[1]{0:T(128)} %bitcast.2.here, s32[321]{0:T(512)} %offsets.1, bf16[1280,1024]{1,0:T(8,128)(2,1)} %coeffs.1, bf16[1280,512]{1,0:T(8,128)(2,1)} %copy-done.6), custom_call_target="tpu_custom_call" | custom-call | tf_op jit(solution)/shard_map/pack_coeffs/pallas_call | solution.py:62
  62.8 5.3 %collective-permute-start.11 = (bf16[960,256]{1,0:T(8,128)(2,1)}, bf16[960,256]{1,0:T(8,128)(2,1)}, u32[]{:S(2)}, u32[]{:S(2)}) collective-permute-start(bf16[960,256]{1,0:T(8,128)(2,1)} %get-tuple-element.34.refs_0_), channel_id=1, source_target_pairs={{0,1},{1,2},{2,3},{4,5},{5,6},{6,7},{8,9},{9,10},{10,11},{12,13},{... | collective-permute-start | bytes 1474568 | tf_op jit(solution)/shard_map/ppermute | solution.py:231
  68.2 38.3 %collective-permute-done.9.refs_1_ = bf16[960,256]{1,0:T(8,128)(2,1)S(1)} collective-permute-done((bf16[960,256]{1,0:T(8,128)(2,1)}, bf16[960,256]{1,0:T(8,128)(2,1)S(1)}, u32[]{:S(2)}, u32[]{:S(2)}) %collective-permute-start.9) | collective-permute-done | bytes 491552 | tf_op jit(solution)/shard_map/ppermute | solution.py:231
  107.8 5.9 %collective-permute-start.7 = (bf16[960,512]{1,0:T(8,128)(2,1)}, bf16[960,512]{1,0:T(8,128)(2,1)}, u32[]{:S(2)}, u32[]{:S(2)}) collective-permute-start(bf16[960,512]{1,0:T(8,128)(2,1)} %get-tuple-element.32.refs_0_), channel_id=1, source_target_pairs={{0,1},{1,2},{2,3},{4,5},{5,6},{6,7},{8,9},{9,10},{10,11},{12,13},{... | collective-permute-start | bytes 2949128 | tf_op jit(solution)/shard_map/ppermute | solution.py:231
  113.7 3.3 %collective-permute-done.11.refs_1_ = bf16[960,256]{1,0:T(8,128)(2,1)} collective-permute-done((bf16[960,256]{1,0:T(8,128)(2,1)}, bf16[960,256]{1,0:T(8,128)(2,1)}, u32[]{:S(2)}, u32[]{:S(2)}) %collective-permute-start.11) | collective-permute-done | bytes 491552 | tf_op jit(solution)/shard_map/ppermute | solution.py:231
  118.4 23.3 %collective-permute-done.17.refs_2_ = bf16[960,256]{1,0:T(8,128)(2,1)} collective-permute-done((bf16[960,256]{1,0:T(8,128)(2,1)}, bf16[960,256]{1,0:T(8,128)(2,1)}, u32[]{:S(2)}, u32[]{:S(2)}) %collective-permute-start.17) | collective-permute-done | bytes 491552 | tf_op jit(solution)/shard_map/ppermute | solution.py:232
  146.7 12.2 %collective-permute-done.16.refs_4_ = bf16[960,256]{1,0:T(8,128)(2,1)S(1)} collective-permute-done((bf16[960,256]{1,0:T(8,128)(2,1)S(1)}, bf16[960,256]{1,0:T(8,128)(2,1)S(1)}, u32[]{:S(2)}, u32[]{:S(2)}) %collective-permute-start.16) | collective-permute-done | bytes 491552 | tf_op jit(solution)/shard_map/ppermute | solution.py:249
  164.3 6.8 %products.6 = (bf16[128,1024]{1,0:T(8,128)(2,1)}, bf16[128,1024]{1,0:T(8,128)(2,1)}, bf16[128,1024]{1,0:T(8,128)(2,1)}, bf16[128,1024]{1,0:T(8,128)(2,1)}) custom-call(s32[4]{0:T(128)} %compare_select_fusion.3.choice, bf16[960,1024]{1,0:T(8,128)(2,1)} %pack_kept.1.kept, bf16[960,1024]{1,0:T(8,128)(2,1)} %copy-done.15, ...), custom_call_target="tpu_custom_call" | custom-call | flops 2013265920 | bytes 3932160 | tf_op jit(solution)/shard_map/products/pallas_call | solution.py:195
  172.7 14.3 %collective-permute-done.18.refs_5_.refs_4_ = bf16[960,256]{1,0:T(8,128)(2,1)S(1)} collective-permute-done((bf16[960,256]{1,0:T(8,128)(2,1)}, bf16[960,256]{1,0:T(8,128)(2,1)S(1)}, u32[]{:S(2)}, u32[]{:S(2)}) %collective-permute-start.18) | collective-permute-done | bytes 491552 | tf_op jit(solution)/shard_map/ppermute | solution.py:249
  187.8 6.8 %products.7 = (bf16[128,1024]{1,0:T(8,128)(2,1)}, bf16[128,1024]{1,0:T(8,128)(2,1)}, bf16[128,1024]{1,0:T(8,128)(2,1)}, bf16[128,1024]{1,0:T(8,128)(2,1)}) custom-call(s32[4]{0:T(128)} %compare_select_fusion.3.choice, bf16[960,1024]{1,0:T(8,128)(2,1)} %pack_kept.1.kept, bf16[960,1024]{1,0:T(8,128)(2,1)} %copy-done.15, ...), custom_call_target="tpu_custom_call" | custom-call | flops 2013265920 | bytes 3932160 | tf_op jit(solution)/shard_map/products/pallas_call | solution.py:195
  194.6 2.2 collective-permute-start.32
  198.2 6.9 %products.4 = (bf16[128,1024]{1,0:T(8,128)(2,1)}, bf16[128,1024]{1,0:T(8,128)(2,1)}, bf16[128,1024]{1,0:T(8,128)(2,1)}, bf16[128,1024]{1,0:T(8,128)(2,1)}) custom-call(s32[4]{0:T(128)} %multiply_add_fusion.choice, bf16[960,1024]{1,0:T(8,128)(2,1)} %collective-permute-done.4.kept, bf16[960,1024]{1,0:T(8,128)(2,1)} %collective-permute-done.5.kept_pair, ...), custom_call_target="tpu_custom_call" | custom-call | flops 2013265920 | bytes 3932160 | tf_op jit(solution)/shard_map/products/pallas_call | solution.py:195
  205.1 2.2 collective-permute-start.35
  207.9 9.7 %products.5 = (bf16[256,1024]{1,0:T(8,128)(2,1)}, bf16[256,1024]{1,0:T(8,128)(2,1)}, bf16[256,1024]{1,0:T(8,128)(2,1)}, bf16[256,1024]{1,0:T(8,128)(2,1)}) custom-call(s32[4]{0:T(128)} %compare_select_fusion.3.choice, bf16[960,1024]{1,0:T(8,128)(2,1)} %pack_kept.1.kept, bf16[960,1024]{1,0:T(8,128)(2,1)} %copy-done.15, ...), custom_call_target="tpu_custom_call" | custom-call | flops 4026531840 | bytes 7864320 | tf_op jit(solution)/shard_map/products/pallas_call | solution.py:195
  222.0 2.2 collective-permute-start.21
  224.5 31.4 %collective-permute-done.20 = bf16[128,1024]{1,0:T(8,128)(2,1)S(1)} collective-permute-done((bf16[128,1024]{1,0:T(8,128)(2,1)}, bf16[128,1024]{1,0:T(8,128)(2,1)S(1)}, u32[]{:S(2)}, u32[]{:S(2)}) %collective-permute-start.20) | collective-permute-done | bytes 262176 | tf_op jit(solution)/shard_map/ppermute | solution.py:287
  261.8 3.5 %collective-permute-done.24 = bf16[128,1024]{1,0:T(8,128)(2,1)S(1)} collective-permute-done((bf16[128,1024]{1,0:T(8,128)(2,1)S(1)}, bf16[128,1024]{1,0:T(8,128)(2,1)S(1)}, u32[]{:S(2)}, u32[]{:S(2)}) %collective-permute-start.24) | collective-permute-done | bytes 262176 | tf_op jit(solution)/shard_map/ppermute | solution.py:296
  266.7 2.2 collective-permute-done.22
  (125 shorter events, 45.7 us)
Async XLA Ops:
  6.6 30.4 %collective-permute-start.1 = (bf16[10,32,1024]{2,1,0:T(8,128)(2,1)}, bf16[10,32,1024]{2,1,0:T(8,128)(2,1)S(1)}, u32[]{:S(2)}, u32[]{:S(2)}) collective-permute-start(bf16[10,32,1024]{2,1,0:T(8,128)(2,1)} %get-tuple-element.30), channel_id=1, source_target_pairs={{0,16},{4,20},{8,24},{12,28},{16,0},{20,4},{24,8},{28,12},{1,17},{... | collective-permute-start | bytes 1966088 | tf_op jit(solution)/shard_map/ppermute | solution.py:240
  6.6 31.3 %collective-permute-start.2 = (bf16[10,32,1024]{2,1,0:T(8,128)(2,1)}, bf16[10,32,1024]{2,1,0:T(8,128)(2,1)S(1)}, u32[]{:S(2)}, u32[]{:S(2)}) collective-permute-start(bf16[10,32,1024]{2,1,0:T(8,128)(2,1)} %get-tuple-element.31), channel_id=1, source_target_pairs={{0,24},{4,28},{8,16},{12,20},{16,8},{20,12},{24,0},{28,4},{1,25},{... | collective-permute-start | bytes 1966088 | tf_op jit(solution)/shard_map/ppermute | solution.py:240
  48.9 69.3 %collective-permute-start.4 = (bf16[960,1024]{1,0:T(8,128)(2,1)}, bf16[960,1024]{1,0:T(8,128)(2,1)}, u32[]{:S(2)}, u32[]{:S(2)}) collective-permute-start(bf16[960,1024]{1,0:T(8,128)(2,1)} %pack_kept.1.kept), channel_id=1, source_target_pairs={{0,1},{3,2},{4,5},{7,6},{8,9},{11,10},{12,13},{15,14},{16,17},{19,... | collective-permute-start | bytes 5898248 | tf_op jit(solution)/shard_map/ppermute | solution.py:251
  60.1 46.3 %collective-permute-start.9 = (bf16[960,256]{1,0:T(8,128)(2,1)}, bf16[960,256]{1,0:T(8,128)(2,1)S(1)}, u32[]{:S(2)}, u32[]{:S(2)}) collective-permute-start(bf16[960,256]{1,0:T(8,128)(2,1)} %get-tuple-element.33.refs_0_), channel_id=1, source_target_pairs={{0,1},{1,2},{2,3},{4,5},{5,6},{6,7},{8,9},{9,10},{10,11},{12,13},{... | collective-permute-start | bytes 1474568 | tf_op jit(solution)/shard_map/ppermute | solution.py:231
  61.5 98.9 %collective-permute-start.26 = (bf16[960,1024]{1,0:T(8,128)(2,1)S(1)}, bf16[960,1024]{1,0:T(8,128)(2,1)S(1)}, u32[]{:S(2)}, u32[]{:S(2)}) collective-permute-start(bf16[960,1024]{1,0:T(8,128)(2,1)S(1)} %copy-done.2), channel_id=1, source_target_pairs={{0,4},{4,0},{8,12},{12,8},{16,20},{20,16},{24,28},{28,24},{1,5},{5... | collective-permute-start | bytes 5898248 | tf_op jit(solution)/shard_map/ppermute | solution.py:246
  61.5 46.2 %collective-permute-start.15 = (bf16[960,256]{1,0:T(8,128)(2,1)}, bf16[960,256]{1,0:T(8,128)(2,1)S(1)}, u32[]{:S(2)}, u32[]{:S(2)}) collective-permute-start(bf16[960,256]{1,0:T(8,128)(2,1)} %get-tuple-element.33.refs_0_), channel_id=1, source_target_pairs={{1,0},{2,1},{3,2},{5,4},{6,5},{7,6},{9,8},{10,9},{11,10},{13,12},{... | collective-permute-start | bytes 1474568 | tf_op jit(solution)/shard_map/ppermute | solution.py:232
  62.8 54.2 %collective-permute-start.11 = (bf16[960,256]{1,0:T(8,128)(2,1)}, bf16[960,256]{1,0:T(8,128)(2,1)}, u32[]{:S(2)}, u32[]{:S(2)}) collective-permute-start(bf16[960,256]{1,0:T(8,128)(2,1)} %get-tuple-element.34.refs_0_), channel_id=1, source_target_pairs={{0,1},{1,2},{2,3},{4,5},{5,6},{6,7},{8,9},{9,10},{10,11},{12,13},{... | collective-permute-start | bytes 1474568 | tf_op jit(solution)/shard_map/ppermute | solution.py:231
  106.5 35.9 %collective-permute-start.13 = (bf16[960,512]{1,0:T(8,128)(2,1)}, bf16[960,512]{1,0:T(8,128)(2,1)}, u32[]{:S(2)}, u32[]{:S(2)}) collective-permute-start(bf16[960,512]{1,0:T(8,128)(2,1)} %get-tuple-element.32.refs_0_), channel_id=1, source_target_pairs={{1,0},{2,1},{3,2},{5,4},{6,5},{7,6},{9,8},{10,9},{11,10},{13,12},{... | collective-permute-start | bytes 2949128 | tf_op jit(solution)/shard_map/ppermute | solution.py:232
  107.8 35.9 %collective-permute-start.7 = (bf16[960,512]{1,0:T(8,128)(2,1)}, bf16[960,512]{1,0:T(8,128)(2,1)}, u32[]{:S(2)}, u32[]{:S(2)}) collective-permute-start(bf16[960,512]{1,0:T(8,128)(2,1)} %get-tuple-element.32.refs_0_), channel_id=1, source_target_pairs={{0,1},{1,2},{2,3},{4,5},{5,6},{6,7},{8,9},{9,10},{10,11},{12,13},{... | collective-permute-start | bytes 2949128 | tf_op jit(solution)/shard_map/ppermute | solution.py:231
  117.0 24.7 %collective-permute-start.17 = (bf16[960,256]{1,0:T(8,128)(2,1)}, bf16[960,256]{1,0:T(8,128)(2,1)}, u32[]{:S(2)}, u32[]{:S(2)}) collective-permute-start(bf16[960,256]{1,0:T(8,128)(2,1)} %get-tuple-element.34.refs_0_), channel_id=1, source_target_pairs={{1,0},{2,1},{3,2},{5,4},{6,5},{7,6},{9,8},{10,9},{11,10},{13,12},{... | collective-permute-start | bytes 1474568 | tf_op jit(solution)/shard_map/ppermute | solution.py:232
  118.3 79.1 %collective-permute-start.5 = (bf16[960,1024]{1,0:T(8,128)(2,1)}, bf16[960,1024]{1,0:T(8,128)(2,1)}, u32[]{:S(2)}, u32[]{:S(2)}) collective-permute-start(bf16[960,1024]{1,0:T(8,128)(2,1)} %collective-permute-done.4.kept), channel_id=1, source_target_pairs={{0,4},{4,0},{8,12},{12,8},{16,20},{20,16},{24,28},{28,24},{1,5},{5... | collective-permute-start | bytes 5898248 | tf_op jit(solution)/shard_map/ppermute | solution.py:252
  143.7 50.9 %collective-permute-start.14 = (bf16[960,512]{1,0:T(8,128)(2,1)}, bf16[960,512]{1,0:T(8,128)(2,1)S(1)}, u32[]{:S(2)}, u32[]{:S(2)}) collective-permute-start(bf16[960,512]{1,0:T(8,128)(2,1)} %collective-permute-done.13.refs_2_), channel_id=1, source_target_pairs={{1,0},{2,1},{5,4},{6,5},{9,8},{10,9},{13,12},{14,13},{17,16},{18,1... | collective-permute-start | bytes 2949128 | tf_op jit(solution)/shard_map/ppermute | solution.py:249
  145.0 51.8 %collective-permute-start.8 = (bf16[960,512]{1,0:T(8,128)(2,1)}, bf16[960,512]{1,0:T(8,128)(2,1)}, u32[]{:S(2)}, u32[]{:S(2)}) collective-permute-start(bf16[960,512]{1,0:T(8,128)(2,1)} %collective-permute-done.7.refs_1_), channel_id=1, source_target_pairs={{1,2},{2,3},{5,6},{6,7},{9,10},{10,11},{13,14},{14,15},{17,18},{18... | collective-permute-start | bytes 2949128 | tf_op jit(solution)/shard_map/ppermute | solution.py:248
  161.7 25.3 %collective-permute-start.18 = (bf16[960,256]{1,0:T(8,128)(2,1)}, bf16[960,256]{1,0:T(8,128)(2,1)S(1)}, u32[]{:S(2)}, u32[]{:S(2)}) collective-permute-start(bf16[960,256]{1,0:T(8,128)(2,1)} %collective-permute-done.17.refs_2_), channel_id=1, source_target_pairs={{1,0},{2,1},{5,4},{6,5},{9,8},{10,9},{13,12},{14,13},{17,16},{18,1... | collective-permute-start | bytes 1474568 | tf_op jit(solution)/shard_map/ppermute | solution.py:249
  171.2 33.9 %collective-permute-start.30 = (bf16[128,1024]{1,0:T(8,128)(2,1)}, bf16[128,1024]{1,0:T(8,128)(2,1)S(1)}, u32[]{:S(2)}, u32[]{:S(2)}) collective-permute-start(bf16[128,1024]{1,0:T(8,128)(2,1)} %get-tuple-element.44), channel_id=1, source_target_pairs={{0,8},{4,12},{8,0},{12,4},{16,24},{20,28},{24,16},{28,20},{1,9},{5... | collective-permute-start | bytes 786440 | tf_op jit(solution)/shard_map/ppermute | solution.py:269
  187.0 20.3 %collective-permute-start.31 = (bf16[128,1024]{1,0:T(8,128)(2,1)}, bf16[128,1024]{1,0:T(8,128)(2,1)S(1)}, u32[]{:S(2)}, u32[]{:S(2)}) collective-permute-start(bf16[128,1024]{1,0:T(8,128)(2,1)} %get-tuple-element.45), channel_id=1, source_target_pairs={{0,16},{4,20},{8,24},{12,28},{16,0},{20,4},{24,8},{28,12},{1,17},{... | collective-permute-start | bytes 786440 | tf_op jit(solution)/shard_map/ppermute | solution.py:269
  194.6 23.0 %collective-permute-start.32 = (bf16[128,1024]{1,0:T(8,128)(2,1)}, bf16[128,1024]{1,0:T(8,128)(2,1)S(1)}, u32[]{:S(2)}, u32[]{:S(2)}) collective-permute-start(bf16[128,1024]{1,0:T(8,128)(2,1)} %get-tuple-element.46), channel_id=1, source_target_pairs={{0,24},{4,28},{8,16},{12,20},{16,8},{20,12},{24,0},{28,4},{1,25},{... | collective-permute-start | bytes 786440 | tf_op jit(solution)/shard_map/ppermute | solution.py:269
  196.9 22.3 %collective-permute-start.33 = (bf16[128,1024]{1,0:T(8,128)(2,1)}, bf16[128,1024]{1,0:T(8,128)(2,1)S(1)}, u32[]{:S(2)}, u32[]{:S(2)}) collective-permute-start(bf16[128,1024]{1,0:T(8,128)(2,1)} %get-tuple-element.48), channel_id=1, source_target_pairs={{0,8},{4,12},{8,0},{12,4},{16,24},{20,28},{24,16},{28,20},{1,9},{5... | collective-permute-start | bytes 786440 | tf_op jit(solution)/shard_map/ppermute | solution.py:269
  197.4 22.6 %collective-permute-start.34 = (bf16[128,1024]{1,0:T(8,128)(2,1)}, bf16[128,1024]{1,0:T(8,128)(2,1)S(1)}, u32[]{:S(2)}, u32[]{:S(2)}) collective-permute-start(bf16[128,1024]{1,0:T(8,128)(2,1)} %get-tuple-element.49), channel_id=1, source_target_pairs={{0,16},{4,20},{8,24},{12,28},{16,0},{20,4},{24,8},{28,12},{1,17},{... | collective-permute-start | bytes 786440 | tf_op jit(solution)/shard_map/ppermute | solution.py:269
  217.7 41.1 %collective-permute-start.27 = (bf16[256,1024]{1,0:T(8,128)(2,1)}, bf16[256,1024]{1,0:T(8,128)(2,1)S(1)}, u32[]{:S(2)}, u32[]{:S(2)}) collective-permute-start(bf16[256,1024]{1,0:T(8,128)(2,1)} %get-tuple-element.40), channel_id=1, source_target_pairs={{0,8},{4,12},{8,0},{12,4},{16,24},{20,28},{24,16},{28,20},{1,9},{5... | collective-permute-start | bytes 1572872 | tf_op jit(solution)/shard_map/ppermute | solution.py:269
  219.2 40.9 %collective-permute-start.28 = (bf16[256,1024]{1,0:T(8,128)(2,1)}, bf16[256,1024]{1,0:T(8,128)(2,1)S(1)}, u32[]{:S(2)}, u32[]{:S(2)}) collective-permute-start(bf16[256,1024]{1,0:T(8,128)(2,1)} %get-tuple-element.41), channel_id=1, source_target_pairs={{0,16},{4,20},{8,24},{12,28},{16,0},{20,4},{24,8},{28,12},{1,17},{... | collective-permute-start | bytes 1572872 | tf_op jit(solution)/shard_map/ppermute | solution.py:269
  220.0 41.4 %collective-permute-start.29 = (bf16[256,1024]{1,0:T(8,128)(2,1)}, bf16[256,1024]{1,0:T(8,128)(2,1)S(1)}, u32[]{:S(2)}, u32[]{:S(2)}) collective-permute-start(bf16[256,1024]{1,0:T(8,128)(2,1)} %get-tuple-element.42), channel_id=1, source_target_pairs={{0,24},{4,28},{8,16},{12,20},{16,8},{20,12},{24,0},{28,4},{1,25},{... | collective-permute-start | bytes 1572872 | tf_op jit(solution)/shard_map/ppermute | solution.py:269
  221.2 34.8 %collective-permute-start.20 = (bf16[128,1024]{1,0:T(8,128)(2,1)}, bf16[128,1024]{1,0:T(8,128)(2,1)S(1)}, u32[]{:S(2)}, u32[]{:S(2)}) collective-permute-start(bf16[128,1024]{1,0:T(8,128)(2,1)} %get-tuple-element.37), channel_id=1, source_target_pairs={{0,16},{4,20},{8,24},{12,28},{16,0},{20,4},{24,8},{28,12},{1,17},{... | collective-permute-start | bytes 786440 | tf_op jit(solution)/shard_map/ppermute | solution.py:287
  222.0 34.0 %collective-permute-start.21 = (bf16[128,1024]{1,0:T(8,128)(2,1)S(1)}, bf16[128,1024]{1,0:T(8,128)(2,1)S(1)}, u32[]{:S(2)}, u32[]{:S(2)}) collective-permute-start(bf16[128,1024]{1,0:T(8,128)(2,1)S(1)} %copy-done.18), channel_id=1, source_target_pairs={{0,24},{4,28},{8,16},{12,20},{16,8},{20,12},{24,0},{28,4},{1,25},{... | collective-permute-start | bytes 786440 | tf_op jit(solution)/shard_map/ppermute | solution.py:287
  (31 other events, 477.8 us)
